TPU v7x, 32 devices: a whole 2x2x4 slice. The times are simulated.
32 devices in a mesh: dp: 8 (over y, x, core), rep: 4 (over z).
Axes of the slice: x: 2, y: 2, z: 4, core: 2. Of those that a mesh axis runs over, the one named last changes fastest.
Arguments:
- student_in: bfloat16 [16384, 320], P(('dp', 'rep')), may hold values from -6 to 6
- target_in: bfloat16 [16384, 320], P(('dp', 'rep')), may hold values from -6 to 6
- timesteps: int32 [64], P(('dp', 'rep')), may hold values from 20 to 999
- student_win: float32 [1280, 320], P('dp'), may hold values from -0.3125 to 0.3125
- student_wout: float32 [640, 320], P('dp'), may hold values from -0.25 to 0.25
- student_wtime: float32 [640, 320], P('dp'), may hold values from -0.25 to 0.25
- student_gain: float32 [320], replicated, may hold values from 0.5 to 1.5
- student_bias: float32 [320], replicated, may hold values from -3 to 3
- target_win: float32 [1280, 320], P('dp'), may hold values from -0.3125 to 0.3125
- target_wout: float32 [640, 320], P('dp'), may hold values from -0.25 to 0.25
- target_wtime: float32 [640, 320], P('dp'), may hold values from -0.25 to 0.25
- target_gain: float32 [320], replicated, may hold values from 0.5 to 1.5
- target_bias: float32 [320], replicated, may hold values from -3 to 3
Outputs:
- grad_win: float32 [1280, 320], P('dp')
- grad_wout: float32 [640, 320], P('dp')
- grad_wtime: float32 [640, 320], P('dp')
- grad_gain: float32 [320], replicated
- grad_bias: float32 [320], replicated
- ema_win: float32 [1280, 320], P('dp')
- ema_wout: float32 [640, 320], P('dp')
- ema_wtime: float32 [640, 320], P('dp')
- ema_gain: float32 [320], replicated
- ema_bias: float32 [320], replicated
Inputs may be any that keep to these rules, and one draw needn't show every extreme that they name: `timesteps`: student timestep of each sample; the target is evaluated at 20 steps earlier.
All inputs are finite; a program needn't handle non-finite values.
Results may differ from a plain program's by a relative error of at most 0.004.
The roundings to bfloat16 on the way count: a program that leaves them out, or rounds other values in their place, can miss the bound.
Values may be sent and summed in bfloat16 or wider, within the bound.
No kernel may reach another device: no remote copies, remote signals or barrier semaphores. Data moves between devices by JAX's collectives and lax.ppermute only.
A program may use at most 64 MiB of HBM per device.

v0:
```python
import math

import jax
import jax.numpy as jnp
from jax import lax
from jax.sharding import PartitionSpec as P

SKIP = 20


ema_decay = 0.95
learn_rate = 0.05


def sinusoid(step_ids, width):
    half_width = width // 2
    frequency = jnp.exp(-math.log(10000.0) * jnp.arange(half_width, dtype=jnp.float32) / half_width)
    angles = step_ids.astype(jnp.float32)[:, None] * frequency[None, :]
    return jnp.concatenate([jnp.cos(angles), jnp.sin(angles)], axis=1)


def gelu_tanh(value):
    inner = 0.7978845608 * (value + 0.044715 * value * value * value)
    return 0.5 * value * (1.0 + jnp.tanh(inner))


def gelu_slope(value):
    tangent = jnp.tanh(0.7978845608 * (value + 0.044715 * value * value * value))
    return 0.5 * (1.0 + tangent) + 0.5 * value * (1.0 - tangent * tangent) * 0.7978845608 * (
        1.0 + 0.134145 * value * value
    )


def contract_last(left, right):
    return lax.dot_general(
        left, right, (((1,), (1,)), ((), ())), preferred_element_type=jnp.float32
    )


def contract_first(left, right):
    return lax.dot_general(
        left, right, (((0,), (0,)), ((), ())), preferred_element_type=jnp.float32
    )


def forward(tok_rows, step_ids, w_in, w_out, w_time, gain, bias):
    time_feat = jax.nn.silu(sinusoid(step_ids, w_time.shape[0])).astype(jnp.bfloat16)
    embedding = jnp.dot(time_feat, w_time, preferred_element_type=jnp.float32)
    samples = step_ids.shape[0]
    width = tok_rows.shape[1]
    summed = tok_rows.astype(jnp.float32).reshape(samples, -1, width) + embedding[:, None, :]
    summed = summed.reshape(-1, width)
    center = summed - jnp.mean(summed, axis=1, keepdims=True)
    inv_std = lax.rsqrt(jnp.mean(center * center, axis=1, keepdims=True) + 1e-05)
    normed = center * inv_std
    normed_b = (normed * gain + bias).astype(jnp.bfloat16)
    mixed = contract_last(normed_b, w_in)
    hidden_count = w_out.shape[0]
    gate_part = mixed[:, :hidden_count]
    up_part = mixed[:, hidden_count:]
    gelu_gate = gelu_tanh(gate_part)
    hidden = (gelu_gate * up_part).astype(jnp.bfloat16)
    output = summed + jnp.dot(hidden, w_out, preferred_element_type=jnp.float32)
    return (output, (time_feat, normed, inv_std, normed_b, gate_part, up_part, gelu_gate, hidden))


def backward(grad_y, saved, w_in, w_out, gain):
    time_feat, normed, inv_std, normed_b, gate_part, up_part, gelu_gate, hidden = saved
    grad_yb = grad_y.astype(jnp.bfloat16)
    grad_h = contract_last(grad_yb, w_out)
    grad_mix = jnp.concatenate(
        [grad_h * up_part * gelu_slope(gate_part), grad_h * gelu_gate], axis=1
    ).astype(jnp.bfloat16)
    grad_z = jnp.dot(grad_mix, w_in, preferred_element_type=jnp.float32)
    grad_gain = jnp.sum(grad_z * normed, axis=0)
    grad_bias = jnp.sum(grad_z, axis=0)
    grad_n = grad_z * gain
    grad_s = grad_y + inv_std * (
        grad_n
        - jnp.mean(grad_n, axis=1, keepdims=True)
        - normed * jnp.mean(grad_n * normed, axis=1, keepdims=True)
    )
    samples = time_feat.shape[0]
    grad_emb = jnp.sum(grad_s.reshape(samples, -1, grad_s.shape[1]), axis=1)
    grad_time = lax.dot_general(
        time_feat.astype(jnp.float32),
        grad_emb,
        (((0,), (0,)), ((), ())),
        precision=lax.Precision.HIGHEST,
        preferred_element_type=jnp.float32,
    )
    return (grad_yb, grad_mix, grad_gain, grad_bias, grad_time)


def fetch(piece_in, piece_out, piece_time):
    return (
        lax.all_gather(piece_in, "dp", axis=0, tiled=True),
        lax.all_gather(piece_out, "dp", axis=0, tiled=True),
        lax.all_gather(piece_time, "dp", axis=0, tiled=True),
    )


def per_device(
    student_in,
    target_in,
    timesteps,
    student_win,
    student_wout,
    student_wtime,
    student_gain,
    student_bias,
    target_win,
    target_wout,
    target_wtime,
    target_gain,
    target_bias,
):
    s_in, s_out, s_time = fetch(
        student_win.astype(jnp.bfloat16),
        student_wout.astype(jnp.bfloat16),
        student_wtime.astype(jnp.bfloat16),
    )
    student_out, saved = forward(
        student_in, timesteps, s_in, s_out, s_time, student_gain, student_bias
    )
    t_in, t_out, t_time = fetch(
        target_win.astype(jnp.bfloat16),
        target_wout.astype(jnp.bfloat16),
        target_wtime.astype(jnp.bfloat16),
    )
    target_out, unused = forward(
        target_in, timesteps - SKIP, t_in, t_out, t_time, target_gain, target_bias
    )
    grad_y = (student_out - target_out) / student_in.shape[0]
    back_in, back_out = (
        lax.all_gather(student_win.astype(jnp.bfloat16), "dp", axis=0, tiled=True),
        lax.all_gather(student_wout.astype(jnp.bfloat16), "dp", axis=0, tiled=True),
    )
    grad_yb, grad_mix, grad_gain, grad_bias, grad_time = backward(
        grad_y, saved, back_in, back_out, student_gain
    )
    normed_b = saved[3]
    hidden = saved[7]
    part = grad_mix
    shard_in = lax.psum_scatter(
        contract_first(part, normed_b), "dp", scatter_dimension=0, tiled=True
    )
    part = hidden
    shard_out = lax.psum_scatter(
        contract_first(part, grad_yb), "dp", scatter_dimension=0, tiled=True
    )
    shard_time = lax.psum_scatter(grad_time, "dp", scatter_dimension=0, tiled=True)
    shard_in, shard_out, shard_time = lax.psum((shard_in, shard_out, shard_time), "rep")
    total_gain, total_bias = lax.psum((grad_gain, grad_bias), ("dp", "rep"))

    def average(target_p, student_p, grad_p):
        return ema_decay * target_p + (1.0 - ema_decay) * (student_p - learn_rate * grad_p)

    return (
        shard_in,
        shard_out,
        shard_time,
        total_gain,
        total_bias,
        average(target_win, student_win, shard_in),
        average(target_wout, student_wout, shard_out),
        average(target_wtime, student_wtime, shard_time),
        average(target_gain, student_gain, total_gain),
        average(target_bias, student_bias, total_bias),
    )


def solution(mesh):
    in_specs = (
        P(("dp", "rep"), None),
        P(("dp", "rep"), None),
        P(("dp", "rep")),
        P("dp", None),
        P("dp", None),
        P("dp", None),
        P(),
        P(),
        P("dp", None),
        P("dp", None),
        P("dp", None),
        P(),
        P(),
    )
    out_specs = (
        P("dp", None),
        P("dp", None),
        P("dp", None),
        P(),
        P(),
        P("dp", None),
        P("dp", None),
        P("dp", None),
        P(),
        P(),
    )
    return jax.shard_map(
        per_device, mesh=mesh, in_specs=in_specs, out_specs=out_specs, check_vma=False
    )
```

profile of v0, /device:TPU:0, one launch (start us, length us, event | category | flops | bytes accessed | tf_op | source)
XLA Modules:
  0.0 256.5 jit_solution(1124549243400351824)
XLA Ops:
  7.2 0.7 fusion.50
  8.0 0.9 convert_element_type.62
  8.9 0.9 convert_element_type.58
  9.8 0.9 convert_element_type.70
  10.7 0.9 convert_element_type.66
  11.6 1.0 convert_element_type.60
  12.6 1.0 convert_element_type.68
  13.6 11.3 %all_gather.22 = bf16[640,320]{1,0:T(8,128)(2,1)S(1)} all-gather(bf16[80,320]{1,0:T(8,128)(2,1)S(1)} %convert_element_type.62), channel_id=1, replica_groups=mesh['dp'=8,'rep'=4] {'dp'}, dimensions={0}, use_global_device_ids=true | all-gather | bytes 460800 | tf_op jit(solution)/shard_map/all_gather | solution.py:98
  24.9 9.8 %all_gather.23 = bf16[640,320]{1,0:T(8,128)(2,1)S(1)} all-gather(bf16[80,320]{1,0:T(8,128)(2,1)S(1)} %convert_element_type.66), channel_id=1, replica_groups=mesh['dp'=8,'rep'=4] {'dp'}, dimensions={0}, use_global_device_ids=true | all-gather | bytes 460800 | tf_op jit(solution)/shard_map/all_gather | solution.py:99
  34.7 8.9 %all_gather.25 = bf16[640,320]{1,0:T(8,128)(2,1)S(1)} all-gather(bf16[80,320]{1,0:T(8,128)(2,1)S(1)} %convert_element_type.70), channel_id=1, replica_groups=mesh['dp'=8,'rep'=4] {'dp'}, dimensions={0}, use_global_device_ids=true | all-gather | bytes 460800 | tf_op jit(solution)/shard_map/all_gather | solution.py:98
  43.6 9.8 %all_gather.20 = bf16[640,320]{1,0:T(8,128)(2,1)S(1)} all-gather(bf16[80,320]{1,0:T(8,128)(2,1)S(1)} %convert_element_type.58), channel_id=1, replica_groups=mesh['dp'=8,'rep'=4] {'dp'}, dimensions={0}, use_global_device_ids=true | all-gather | bytes 460800 | tf_op jit(solution)/shard_map/all_gather | solution.py:99
  56.1 10.0 %all_gather.21 = bf16[1280,320]{1,0:T(8,128)(2,1)S(1)} all-gather(bf16[160,320]{1,0:T(8,128)(2,1)S(1)} %convert_element_type.60), channel_id=1, replica_groups=mesh['dp'=8,'rep'=4] {'dp'}, dimensions={0}, use_global_device_ids=true | all-gather | bytes 921600 | tf_op jit(solution)/shard_map/all_gather | solution.py:97
  66.1 10.9 %all_gather.24 = bf16[1280,320]{1,0:T(8,128)(2,1)S(1)} all-gather(bf16[160,320]{1,0:T(8,128)(2,1)S(1)} %convert_element_type.68), channel_id=1, replica_groups=mesh['dp'=8,'rep'=4] {'dp'}, dimensions={0}, use_global_device_ids=true | all-gather | bytes 921600 | tf_op jit(solution)/shard_map/all_gather | solution.py:97
  77.0 1.0 fusion.48
  78.7 1.0 fusion.21
  79.8 0.7 convolution_add_fusion
  81.0 0.8 copy-done
  81.9 1.5 fusion.26
  83.6 2.6 %fusion.12 = (bf16[512,640]{1,0:T(8,128)(2,1)S(1)}, bf16[512,640]{1,0:T(8,128)(2,1)S(1)}) fusion(f32[512,1280]{1,0:T(8,128)S(1)} %fusion.48, bf16[640,320]{1,0:T(8,128)(2,1)} %copy-done.5, f32[512,320]{0,1:T(8,128)} %copy-done), kind=kOutput, calls=%fused_computation.15 | convolution fusion | flops 217415680 | bytes 4997120 | tf_op jit(solution)/shard_map/dot_general | solution.py:35
  86.3 0.9 multiply_reduce_fusion
  88.9 1.6 fusion.44
  90.7 2.2 fusion.16
  93.0 26.5 %reduce-scatter.6.cloned.1.call-done = f32[80,320]{1,0:T(8,128)} async-done(((f32[640,320]{1,0:T(8,128)}), f32[80,320]{1,0:T(8,128)}) %reduce-scatter.6.cloned.1.call-update) | async-done | bytes 102416 | tf_op jit(solution)/shard_map/reduce_scatter | solution.py:149
  119.5 39.0 %reduce-scatter.8.cloned.1.call-done = f32[80,320]{1,0:T(8,128)} async-done(((f32[640,320]{1,0:T(8,128)}), f32[80,320]{1,0:T(8,128)}) %reduce-scatter.8.cloned.1.call-update) | async-done | bytes 102416 | tf_op jit(solution)/shard_map/reduce_scatter | solution.py:152
  158.5 43.6 %reduce-scatter.4.cloned.1.call-done = f32[160,320]{1,0:T(8,128)} async-done(((f32[1280,320]{1,0:T(8,128)}), f32[160,320]{1,0:T(8,128)}) %reduce-scatter.4.cloned.1.call-update) | async-done | bytes 204816 | tf_op jit(solution)/shard_map/reduce_scatter | solution.py:145
  202.1 39.6 %all-reduce = (f32[320]{0:T(512)S(1)}, f32[320]{0:T(512)S(1)}) all-reduce(f32[320]{0:T(512)S(1)} %get-tuple-element.10, f32[320]{0:T(512)S(1)} %get-tuple-element.13), channel_id=1, replica_groups=mesh['dp'=8,'rep'=4] {'dp','rep'}, use_global_device_ids=true, to_apply=%region_14.15 | all-reduce | flops 640 | bytes 5120 | tf_op jit(solution)/shard_map/psum | solution.py:154
  242.3 0.7 all-reduce.4.cloned.1.call-done
  243.0 1.6 multiply_add_fusion.5
  244.6 1.6 multiply_add_fusion.4
  246.2 1.7 multiply_add_fusion.3
  247.9 0.7 copy.34
  249.3 0.6 copy.36
  (83 shorter events, 7.2 us)
Async XLA Ops:
  7.2 112.4 %reduce-scatter.6.cloned.1.call-start = ((), (), s32[]{:S(2)}) async-start(), calls=%async_computation.4 | async-start | bytes 1105920 | tf_op jit(solution)/shard_map/reduce_scatter | solution.py:149
  24.9 55.6 %copy-start.5 = (bf16[640,320]{1,0:T(8,128)(2,1)}, bf16[640,320]{1,0:T(8,128)(2,1)S(1)}, u32[]{:S(2)}) copy-start(bf16[640,320]{1,0:T(8,128)(2,1)S(1)} %all_gather.22) | copy-start | bytes 1228804
  53.5 1.0 copy-start.15
  54.8 1.0 copy-start.4
  56.1 21.0 %copy-start.16 = (f32[320]{0:T(512)S(1)}, f32[320]{0:T(512)}, u32[]{:S(2)}) copy-start(f32[320]{0:T(512)} %param.19) | copy-start | bytes 3844
  56.1 21.0 %copy-start.17 = (f32[320]{0:T(512)S(1)}, f32[320]{0:T(512)}, u32[]{:S(2)}) copy-start(f32[320]{0:T(512)} %param.20) | copy-start | bytes 3844
  66.1 10.9 %copy-start.2 = (bf16[1280,320]{1,0:T(8,128)(2,1)}, bf16[1280,320]{1,0:T(8,128)(2,1)S(1)}, u32[]{:S(2)}) copy-start(bf16[1280,320]{1,0:T(8,128)(2,1)S(1)} %all_gather.21) | copy-start | bytes 2457604
  78.0 0.7 copy-start.18
  78.1 0.7 copy-start.19
  81.0 0.8 copy-start
  83.4 75.1 %reduce-scatter.8.cloned.1.call-start = ((), (), s32[]{:S(2)}) async-start(), calls=%async_computation.5 | async-start | bytes 1105920 | tf_op jit(solution)/shard_map/reduce_scatter | solution.py:152
  83.6 2.7 %copy-start.3 = (bf16[1280,320]{1,0:T(8,128)(2,1)S(1)}, bf16[1280,320]{1,0:T(8,128)(2,1)}, u32[]{:S(2)}) copy-start(bf16[1280,320]{1,0:T(8,128)(2,1)} %copy-done.2) | copy-start | bytes 2457604
  86.3 0.9 copy-start.22
  86.3 1.0 copy-start.24
  86.3 1.6 copy-start.1
  88.5 2.1 copy-start.23
  88.9 1.7 copy-start.25
  90.6 111.5 %reduce-scatter.4.cloned.1.call-start = ((), (), s32[]{:S(2)}) async-start(), calls=%async_computation.3 | async-start | bytes 2211840 | tf_op jit(solution)/shard_map/reduce_scatter | solution.py:145
  92.9 150.1 %copy-start.9 = (f32[80,320]{1,0:T(8,128)S(1)}, f32[80,320]{1,0:T(8,128)}, u32[]{:S(2)}) copy-start(f32[80,320]{1,0:T(8,128)} %param.22) | copy-start | bytes 307204
  92.9 150.1 %copy-start.10 = (f32[80,320]{1,0:T(8,128)S(1)}, f32[80,320]{1,0:T(8,128)}, u32[]{:S(2)}) copy-start(f32[80,320]{1,0:T(8,128)} %param.17) | copy-start | bytes 307204
  92.9 151.7 %copy-start.11 = (f32[80,320]{1,0:T(8,128)S(1)}, f32[80,320]{1,0:T(8,128)}, u32[]{:S(2)}) copy-start(f32[80,320]{1,0:T(8,128)} %param.18) | copy-start | bytes 307204
  92.9 151.7 %copy-start.12 = (f32[80,320]{1,0:T(8,128)S(1)}, f32[80,320]{1,0:T(8,128)}, u32[]{:S(2)}) copy-start(f32[80,320]{1,0:T(8,128)} %param.23) | copy-start | bytes 307204
  92.9 153.3 %copy-start.6 = (f32[160,320]{1,0:T(8,128)S(1)}, f32[160,320]{1,0:T(8,128)}, u32[]{:S(2)}) copy-start(f32[160,320]{1,0:T(8,128)} %param.16) | copy-start | bytes 614404
  92.9 153.3 %copy-start.7 = (f32[160,320]{1,0:T(8,128)S(1)}, f32[160,320]{1,0:T(8,128)}, u32[]{:S(2)}) copy-start(f32[160,320]{1,0:T(8,128)} %param.21) | copy-start | bytes 614404
  93.0 150.0 %all-reduce.4.cloned.1.call-start = ((), (), s32[]{:S(2)}) async-start(), calls=%async_computation.6 | async-start | bytes 983040 | tf_op jit(solution)/shard_map/psum | solution.py:153
  241.7 7.6 %copy-start.20 = (f32[320]{0:T(512)}, f32[320]{0:T(512)S(1)}, u32[]{:S(2)}) copy-start(f32[320]{0:T(512)S(1)} %get-tuple-element.39) | copy-start | bytes 3844
  241.7 7.6 %copy-start.21 = (f32[320]{0:T(512)}, f32[320]{0:T(512)S(1)}, u32[]{:S(2)}) copy-start(f32[320]{0:T(512)S(1)} %get-tuple-element.40) | copy-start | bytes 3844
  243.0 4.9 %copy-start.8 = (f32[160,320]{1,0:T(8,128)S(1)}, f32[160,320]{1,0:T(8,128)}, u32[]{:S(2)}) copy-start(f32[160,320]{1,0:T(8,128)} %get-tuple-element.36) | copy-start | bytes 614404
  243.0 5.6 %copy-start.14 = (f32[80,320]{1,0:T(8,128)S(1)}, f32[80,320]{1,0:T(8,128)}, u32[]{:S(2)}) copy-start(f32[80,320]{1,0:T(8,128)} %get-tuple-element.37) | copy-start | bytes 307204
  243.0 6.3 %copy-start.13 = (f32[80,320]{1,0:T(8,128)S(1)}, f32[80,320]{1,0:T(8,128)}, u32[]{:S(2)}) copy-start(f32[80,320]{1,0:T(8,128)} %get-tuple-element.38) | copy-start | bytes 307204
Sparse Core Ops, SparseCore 0:
  83.5 35.9 reduce-scatter.5
  122.8 35.7 reduce-scatter.7
  161.9 40.1 reduce-scatter.3
  204.5 38.4 all-reduce.3
where the time goes:
time: 257 us; the launch traced here: 256 us
  waiting for transfers between devices  110 us (43%)
  blocking collectives  100 us (39%)
  between operations  14.1 us (5%)
  other arithmetic  13.6 us (5%)
  matrix products  12.8 us (5%)
  local copies, waits for them, and re-layouts  5.4 us (2%)
    reduce_scatter x1, waiting for transfers between devices, per_device(): lax.psum_scatter(contract_first(part, normed_b), 'dp', scatter_dimension=...  43.6 us
    psum x1, blocking collectives, per_device(): total_gain, total_bias = lax.psum((grad_gain, grad_bias), ('dp', 'rep'))  39.6 us
    reduce_scatter x1, waiting for transfers between devices, per_device(): lax.psum_scatter(grad_time, 'dp', scatter_dimension=0, tiled=True)  39 us
    reduce_scatter x1, waiting for transfers between devices, per_device(): lax.psum_scatter(contract_first(part, grad_yb), 'dp', scatter_dimension=0...  26.5 us
    all_gather x2, blocking collectives, fetch(): lax.all_gather(piece_in, 'dp', axis=0, tiled=True)  20.9 us
    all_gather x2, blocking collectives, fetch(): lax.all_gather(piece_out, 'dp', axis=0, tiled=True)  20.2 us
    all_gather x2, blocking collectives, fetch(): lax.all_gather(piece_time, 'dp', axis=0, tiled=True)  19.6 us
    add x4, other arithmetic, average(): ema_decay * target_p + (1.0 - ema_decay) * (student_p - learn_rate * grad_p)  5.5 us
  transfers between devices with their start and end apart: 4, of which 4 were waited for; matrix products, arithmetic and copies ran while one was open for 4% of the time, Pallas kernels for 0%

commit v1 on v0

v1 whole, which is shorter than its diff:
```python
import math

import jax
import jax.numpy as jnp
from jax import lax
from jax.sharding import PartitionSpec as P

SKIP = 20


ema_decay = 0.95
learn_rate = 0.05


def gelu_tanh(value):
    inner = 0.7978845608 * (value + 0.044715 * value * value * value)
    return 0.5 * value * (1.0 + jnp.tanh(inner))


def gelu_slope(value):
    tangent = jnp.tanh(0.7978845608 * (value + 0.044715 * value * value * value))
    return 0.5 * (1.0 + tangent) + 0.5 * value * (1.0 - tangent * tangent) * 0.7978845608 * (
        1.0 + 0.134145 * value * value
    )


def contract_last(left, right):
    return lax.dot_general(
        left, right, (((1,), (1,)), ((), ())), preferred_element_type=jnp.float32
    )


def contract_first(left, right):
    return lax.dot_general(
        left, right, (((0,), (0,)), ((), ())), preferred_element_type=jnp.float32
    )


def tree_sum(parts):
    parts = list(parts)
    while len(parts) > 1:
        parts = [parts[i] + parts[i + 1] for i in range(0, len(parts) - 1, 2)] + parts[len(parts) - len(parts) % 2 :]
    return parts[0]


def exchange(x, axis, count, mask):
    return lax.ppermute(x, axis, [(i, i ^ mask) for i in range(count)])


def gather_rows(x, count, order):
    me = lax.axis_index("dp")
    done = []
    for bit in order:
        other = exchange(x, "dp", count, 1 << bit)
        mine_is_high = ((me >> bit) & 1) == 1
        low = jnp.where(mine_is_high, other, x)
        high = jnp.where(mine_is_high, x, other)
        x = jnp.stack([low, high], axis=sum(1 for b in done if b > bit))
        done.append(bit)
    return x


def gather_small(x, axis, count):
    return [x] + [exchange(x, axis, count, k) for k in range(1, count)]


def scatter_small(parts, count):
    kept = [parts[j] for j in range(0, count, 2)]
    sent = jnp.stack([parts[j + 1] for j in range(0, count, 2)])
    sent = exchange(sent, "dp", count, 1)
    kept = [kept[m] + sent[m] for m in range(count // 2)]
    return tree_sum([kept[0]] + [exchange(kept[m], "dp", count, 2 * m) for m in range(1, count // 2)])


def scatter_blocks(blocks, count):
    me = lax.axis_index("dp")
    core = me & 1
    pairs = blocks.reshape((count // 2, 2) + blocks.shape[1:])
    away = lax.dynamic_index_in_dim(pairs, 1 - core, axis=1, keepdims=False)
    keep = lax.dynamic_index_in_dim(pairs, core, axis=1, keepdims=False)
    chip = me >> 1
    keep = keep + exchange(away.astype(CORE_TYPE), "dp", count, 1).astype(jnp.float32)
    total = lax.dynamic_index_in_dim(keep, chip, axis=0, keepdims=False)
    for k in range(1, count // 2):
        part = lax.dynamic_index_in_dim(keep, chip ^ k, axis=0, keepdims=False).astype(jnp.bfloat16)
        total = total + exchange(part, "dp", count, 2 * k).astype(jnp.float32)
    return total


def sum_over_rep(x, count):
    me = lax.axis_index("rep")
    rows = x.shape[0] // count
    chunks = x.reshape((count, rows) + x.shape[1:])
    total = lax.dynamic_index_in_dim(chunks, me, axis=0, keepdims=False)
    for k in range(1, count):
        part = lax.dynamic_index_in_dim(chunks, me ^ k, axis=0, keepdims=False).astype(jnp.bfloat16)
        total = total + exchange(part, "rep", count, k).astype(jnp.float32)
    total = total.astype(jnp.bfloat16)
    got = gather_small(total, "rep", count)
    out = jnp.zeros((count, rows) + x.shape[1:], jnp.bfloat16)
    for k in range(count):
        out = lax.dynamic_update_index_in_dim(out, got[k], me ^ k, axis=0)
    return out.reshape(x.shape).astype(jnp.float32)


CORE_TYPE = jnp.bfloat16


def time_features(step_ids, rows, width):
    half_width = width // 2
    column = lax.axis_index("dp") * rows + jnp.arange(rows)
    is_cos = column < half_width
    index = jnp.where(is_cos, column, column - half_width).astype(jnp.float32)
    frequency = jnp.exp(-math.log(10000.0) * index / half_width)
    angles = step_ids.astype(jnp.float32)[:, None] * frequency[None, :]
    wave = jnp.where(is_cos[None, :], jnp.cos(angles), jnp.sin(angles))
    return jax.nn.silu(wave).astype(jnp.bfloat16)


def normalize(tok_rows, embedding, gain, bias):
    samples, width = embedding.shape
    summed = tok_rows.astype(jnp.float32).reshape(samples, -1, width) + embedding[:, None, :]
    summed = summed.reshape(-1, width)
    center = summed - jnp.mean(summed, axis=1, keepdims=True)
    inv_std = lax.rsqrt(jnp.mean(center * center, axis=1, keepdims=True) + 1e-05)
    normed = center * inv_std
    return summed, normed, inv_std, (normed * gain + bias).astype(jnp.bfloat16)


def make_per_device(n_dp, n_rep):
    paired = n_dp <= 8
    bits = n_dp.bit_length() - 1

    def gather_net(win, wout, order):
        rows = win.shape[0]
        width = win.shape[1]
        if not paired:
            return (
                lax.all_gather(win.astype(jnp.bfloat16), "dp", axis=0, tiled=True),
                lax.all_gather(wout.astype(jnp.bfloat16), "dp", axis=0, tiled=True),
            )
        both = jnp.concatenate([win.astype(jnp.bfloat16), wout.astype(jnp.bfloat16)])
        full = gather_rows(both, n_dp, order)
        full = full.reshape((n_dp,) + both.shape)
        return full[:, :rows].reshape(-1, width), full[:, rows:].reshape(-1, width)

    def per_device(
        student_in,
        target_in,
        timesteps,
        student_win,
        student_wout,
        student_wtime,
        student_gain,
        student_bias,
        target_win,
        target_wout,
        target_wtime,
        target_gain,
        target_bias,
    ):
        width = student_in.shape[1]
        samples = timesteps.shape[0]
        up = list(range(1, bits)) + [0]
        down = list(range(bits - 1, 0, -1)) + [0]
        if paired:
            ids = jnp.stack(gather_small(timesteps, "dp", n_dp)).reshape(-1)
        else:
            ids = lax.all_gather(timesteps, "dp", axis=0, tiled=True)
        s_in, s_out = gather_net(student_win, student_wout, up)
        t_in, t_out = gather_net(target_win, target_wout, down)
        t_rows = student_wtime.shape[0]
        s_feat = time_features(ids, t_rows, t_rows * n_dp)
        t_feat = time_features(ids - SKIP, t_rows, t_rows * n_dp)
        s_emb = jnp.dot(s_feat, student_wtime.astype(jnp.bfloat16), preferred_element_type=jnp.float32)
        t_emb = jnp.dot(t_feat, target_wtime.astype(jnp.bfloat16), preferred_element_type=jnp.float32)
        both = jnp.concatenate([s_emb.reshape(n_dp, samples, width), t_emb.reshape(n_dp, samples, width)], axis=1)
        if paired:
            both = scatter_small([both[j] for j in range(n_dp)], n_dp)
        else:
            both = lax.psum_scatter(both, "dp", scatter_dimension=0, tiled=True)[0]

        s_sum, normed, inv_std, normed_b = normalize(student_in, both[:samples], student_gain, student_bias)
        t_sum, _, _, t_normed_b = normalize(target_in, both[samples:], target_gain, target_bias)
        hidden_count = s_out.shape[0]
        mixed = contract_last(normed_b, s_in)
        gate_part = mixed[:, :hidden_count]
        up_part = mixed[:, hidden_count:]
        gelu_gate = gelu_tanh(gate_part)
        hidden = (gelu_gate * up_part).astype(jnp.bfloat16)
        student_out = s_sum + jnp.dot(hidden, s_out, preferred_element_type=jnp.float32)
        t_mixed = contract_last(t_normed_b, t_in)
        t_hidden = (gelu_tanh(t_mixed[:, :hidden_count]) * t_mixed[:, hidden_count:]).astype(jnp.bfloat16)
        target_out = t_sum + jnp.dot(t_hidden, t_out, preferred_element_type=jnp.float32)
        grad_y = (student_out - target_out) / student_in.shape[0]

        grad_yb = grad_y.astype(jnp.bfloat16)
        grad_wout = contract_first(hidden, grad_yb)
        grad_h = contract_last(grad_yb, s_out)
        grad_mix = jnp.concatenate(
            [grad_h * up_part * gelu_slope(gate_part), grad_h * gelu_gate], axis=1
        ).astype(jnp.bfloat16)
        grad_win = contract_first(grad_mix, normed_b)
        if paired:
            blocks = jnp.concatenate(
                [grad_win.reshape(n_dp, -1, width), grad_wout.reshape(n_dp, -1, width)], axis=1
            )
            shard = scatter_blocks(blocks, n_dp)
        else:
            shard = jnp.concatenate(
                [
                    lax.psum_scatter(grad_win, "dp", scatter_dimension=0, tiled=True),
                    lax.psum_scatter(grad_wout, "dp", scatter_dimension=0, tiled=True),
                ]
            )
        grad_z = jnp.dot(grad_mix, s_in, preferred_element_type=jnp.float32)
        grad_gain = jnp.sum(grad_z * normed, axis=0)
        grad_bias = jnp.sum(grad_z, axis=0)
        grad_n = grad_z * student_gain
        grad_s = grad_y + inv_std * (
            grad_n
            - jnp.mean(grad_n, axis=1, keepdims=True)
            - normed * jnp.mean(grad_n * normed, axis=1, keepdims=True)
        )
        grad_emb = jnp.sum(grad_s.reshape(samples, -1, width), axis=1)
        small = jnp.concatenate([grad_emb, grad_gain[None], grad_bias[None]])
        if paired:
            smalls = gather_small(small, "dp", n_dp)
        else:
            every = lax.all_gather(small, "dp")
            smalls = [every[j] for j in range(n_dp)]
        embs = jnp.stack([s[:samples] for s in smalls]).reshape(-1, width)
        grad_time = lax.dot_general(
            s_feat.astype(jnp.float32),
            embs,
            (((0,), (0,)), ((), ())),
            precision=lax.Precision.HIGHEST,
            preferred_element_type=jnp.float32,
        )
        affine = tree_sum([s[samples:] for s in smalls])
        affine = tree_sum(gather_small(affine, "rep", n_rep))
        total_gain, total_bias = affine[0], affine[1]
        joined = jnp.concatenate([shard, grad_time])
        if joined.shape[0] % (16 * n_rep) == 0 and paired:
            joined = sum_over_rep(joined, n_rep)
        else:
            joined = lax.psum(joined, "rep")
        in_rows = student_win.shape[0]
        out_rows = student_wout.shape[0]
        shard_in = joined[:in_rows]
        shard_out = joined[in_rows : in_rows + out_rows]
        shard_time = joined[in_rows + out_rows :]

        def average(target_p, student_p, grad_p):
            return ema_decay * target_p + (1.0 - ema_decay) * (student_p - learn_rate * grad_p)

        return (
            shard_in,
            shard_out,
            shard_time,
            total_gain,
            total_bias,
            average(target_win, student_win, shard_in),
            average(target_wout, student_wout, shard_out),
            average(target_wtime, student_wtime, shard_time),
            average(target_gain, student_gain, total_gain),
            average(target_bias, student_bias, total_bias),
        )

    return per_device


def solution(mesh):
    in_specs = (
        P(("dp", "rep"), None),
        P(("dp", "rep"), None),
        P(("dp", "rep")),
        P("dp", None),
        P("dp", None),
        P("dp", None),
        P(),
        P(),
        P("dp", None),
        P("dp", None),
        P("dp", None),
        P(),
        P(),
    )
    out_specs = (
        P("dp", None),
        P("dp", None),
        P("dp", None),
        P(),
        P(),
        P("dp", None),
        P("dp", None),
        P("dp", None),
        P(),
        P(),
    )
    return jax.shard_map(
        make_per_device(mesh.shape["dp"], mesh.shape["rep"]), mesh=mesh, in_specs=in_specs, out_specs=out_specs, check_vma=False
    )
```

time: 257 us -> 159 us (0.62)
  blocking collectives: 100 us -> 0 us
  waiting for transfers between devices: 110 us -> 31.1 us
  local copies, waits for them, and re-layouts: 5.4 us -> 44.7 us
  starting transfers between devices: 0.34 us -> 39.6 us
  other arithmetic: 13.6 us -> 28.5 us
  between operations: 14.1 us -> 1.42 us
    reduce_scatter x3 -> x0, waiting for transfers between devices: 109 us -> none  [the longest x1 43.6 us: per_device(): lax.psum_scatter(contract_first(part, normed_b), 'dp', scatter_dimension=...]
    all_gather x6 -> x0, blocking collectives: 60.7 us -> none  [the longest x2 20.9 us: fetch(): lax.all_gather(piece_in, 'dp', axis=0, tiled=True)]
    ppermute x0 -> x37, starting transfers between devices: none -> 39.6 us  [exchange(): return lax.ppermute(x, axis, [(i, i ^ mask) for i in range(count)])]
    psum x1 -> x0, blocking collectives: 39.6 us -> none  [per_device(): total_gain, total_bias = lax.psum((grad_gain, grad_bias), ('dp', 'rep'))]
    ppermute x0 -> x37, waiting for transfers between devices: none -> 31.1 us  [exchange(): return lax.ppermute(x, axis, [(i, i ^ mask) for i in range(count)])]
    slice x0 -> x17, local copies, waits for them, and re-layouts: none -> 15.1 us  [the longest x6 7.16 us: per_device(): affine = tree_sum([s[samples:] for s in smalls])]
    another operation x0 -> x12, other arithmetic: none -> 11.9 us  [the longest x11 11.9 us: gather_rows(): x = jnp.stack([low, high], axis=sum((1 for b in done if b > bit)))]
    another operation x0 -> x15, local copies, waits for them, and re-layouts: none -> 9.65 us  [the longest x4 6.76 us: gather_rows(): x = jnp.stack([low, high], axis=sum((1 for b in done if b > bit)))]
  transfers between devices with their start and end apart: 4 -> 37, of which waited for: 4 -> 15; matrix products, arithmetic and copies ran while one was open for 4% -> 29% of each run, Pallas kernels for 0% -> 0%
where the time goes in v1:
time: 159 us; the launch traced here: 157 us
  local copies, waits for them, and re-layouts  44.7 us (28%)
  starting transfers between devices  39.6 us (25%)
  waiting for transfers between devices  31.1 us (20%)
  other arithmetic  28.5 us (18%)
  matrix products  12.2 us (8%)
    ppermute x37, starting transfers between devices, exchange(): return lax.ppermute(x, axis, [(i, i ^ mask) for i in range(count)])  39.6 us
    ppermute x37, waiting for transfers between devices, exchange(): return lax.ppermute(x, axis, [(i, i ^ mask) for i in range(count)])  31.1 us
    another operation x11, other arithmetic, gather_rows(): x = jnp.stack([low, high], axis=sum((1 for b in done if b > bit)))  11.9 us
    slice x6, local copies, waits for them, and re-layouts, per_device(): affine = tree_sum([s[samples:] for s in smalls])  7.16 us
    unnamed x63, local copies, waits for them, and re-layouts  7.09 us
    another operation x4, local copies, waits for them, and re-layouts, gather_rows(): x = jnp.stack([low, high], axis=sum((1 for b in done if b > bit)))  6.76 us
    dot_general x3, matrix products, contract_last(): lax.dot_general(left, right, (((1,), (1,)), ((), ())), preferred_element_...  4.55 us
    slice x4, local copies, waits for them, and re-layouts, gather_net(): full[:, rows:].reshape(-1, width)  4.52 us
  transfers between devices with their start and end apart: 37, of which 15 were waited for; matrix products, arithmetic and copies ran while one was open for 29% of the time, Pallas kernels for 0%

profile of v1, /device:TPU:0, one launch (start us, length us, event | category | flops | bytes accessed | tf_op | source)
XLA Modules:
  0.0 157.5 jit_solution(16296277338963171141)
XLA Ops:
  0.7 2.5 %collective-permute-start.4 = (s32[2]{0:T(128)}, s32[2]{0:T(128)S(1)}, u32[]{:S(2)}, u32[]{:S(2)}) collective-permute-start(s32[2]{0:T(128)} %param.15), channel_id=1, source_target_pairs={{0,20},{4,16},{8,28},{12,24},{16,4},{20,0},{24,12},{28,8},{1,21},{... | collective-permute-start | bytes 32 | tf_op jit(solution)/shard_map/ppermute | solution.py:47
  8.3 2.7 %collective-permute-start.6 = (s32[2]{0:T(128)}, s32[2]{0:T(128)S(1)}, u32[]{:S(2)}, u32[]{:S(2)}) collective-permute-start(s32[2]{0:T(128)} %param.15), channel_id=1, source_target_pairs={{0,28},{4,24},{8,20},{12,16},{16,12},{20,8},{24,4},{28,0},{1,29},{... | collective-permute-start | bytes 32 | tf_op jit(solution)/shard_map/ppermute | solution.py:47
  12.5 3.2 %collective-permute-done.5 = s32[2]{0:T(128)S(1)} collective-permute-done((s32[2]{0:T(128)}, s32[2]{0:T(128)S(1)}, u32[]{:S(2)}, u32[]{:S(2)}) %collective-permute-start.5) | collective-permute-done | bytes 40 | tf_op jit(solution)/shard_map/ppermute | solution.py:47
  24.7 2.2 %collective-permute-done.10 = f32[4,320]{1,0:T(4,128)S(1)} collective-permute-done((f32[4,320]{1,0:T(4,128)S(1)}, f32[4,320]{1,0:T(4,128)S(1)}, u32[]{:S(2)}, u32[]{:S(2)}) %collective-permute-start.10) | collective-permute-done | bytes 5152 | tf_op jit(solution)/shard_map/ppermute | solution.py:47
  35.5 5.3 %collective-permute-done.15 = bf16[2,240,320]{2,1,0:T(8,128)(2,1)S(1)} collective-permute-done((bf16[2,240,320]{2,1,0:T(8,128)(2,1)S(1)}, bf16[2,240,320]{2,1,0:T(8,128)(2,1)S(1)}, u32[]{:S(2)}, u32[]{:S(2)}) %collective-permute-start.15) | collective-permute-done | bytes 307232 | tf_op jit(solution)/shard_map/ppermute | solution.py:47
  42.2 1.8 %collective-permute-done.12 = bf16[2,240,320]{2,1,0:T(8,128)(2,1)} collective-permute-done((bf16[2,240,320]{2,1,0:T(8,128)(2,1)}, bf16[2,240,320]{2,1,0:T(8,128)(2,1)}, u32[]{:S(2)}, u32[]{:S(2)}) %collective-permute-start.12) | collective-permute-done | bytes 307232 | tf_op jit(solution)/shard_map/ppermute | solution.py:47
  46.1 2.2 %copy.279 = bf16[2,2,240,320]{2,3,1,0:T(8,128)(2,1)} copy(bf16[2,2,240,320]{3,2,1,0:T(8,128)(2,1)} %pad_maximum_fusion.4) | data formatting | bytes 1228800 | tf_op jit(solution)/shard_map/stack | solution.py:58
  48.6 2.2 %copy.288 = bf16[2,2,240,320]{3,2,1,0:T(8,128)(2,1)} copy(bf16[2,2,240,320]{2,3,1,0:T(8,128)(2,1)} %collective-permute-done.16) | data formatting | bytes 1228800 | tf_op jit(solution)/shard_map/ppermute | solution.py:47
  50.9 2.2 %copy.280 = bf16[2,2,240,320]{3,2,1,0:T(8,128)(2,1)} copy(bf16[2,2,240,320]{2,3,1,0:T(8,128)(2,1)} %collective-permute-done.13) | data formatting | bytes 1228800 | tf_op jit(solution)/shard_map/ppermute | solution.py:47
  53.1 2.7 %select_bitcast_fusion.1 = (bf16[2,2,1,240,320]{4,3,1,0,2:T(8,128)(2,1)S(1)}, bf16[2,2,1,240,320]{4,3,1,0,2:T(8,128)(2,1)S(1)}, bf16[2,2,1,240,320]{4,3,1,0,2:T(8,128)(2,1)S(1)}, bf16[2,2,1,240,320]{4,3,1,0,2:T(8,128)(2,1)}) fusion(bf16[2,2,240,320]{3,2,1,0:T(8,128)(2,1)} %copy.288, pred[]{:T(512)S(6)} %eq.12, ...), kind=kLoop, calls=%fused_computation.40 | loop fusion | flops 1843200 | bytes 4915201 | tf_op jit(solution)/shard_map/stack | solution.py:58
  57.2 1.7 %copy.290 = bf16[2,2,2,240,320]{3,4,2,1,0:T(8,128)(2,1)S(1)} copy(bf16[2,2,2,240,320]{4,3,1,0,2:T(8,128)(2,1)} %pad_maximum_fusion.1) | data formatting | bytes 2457600 | tf_op jit(solution)/shard_map/stack | solution.py:58
  60.0 2.1 %copy.292 = bf16[8,80,320]{2,1,0:T(8,128)(2,1)} copy(bf16[8,80,320]{1,2,0:T(8,128)(2,1)} %slice.205) | data formatting | bytes 819200 | tf_op jit(solution)/shard_map/slice | solution.py:145
  63.6 2.5 %pad_maximum_fusion = bf16[2,2,2,240,320]{4,3,1,0,2:T(8,128)(2,1)} fusion(bf16[2,2,1,240,320]{4,3,1,0,2:T(8,128)(2,1)S(1)} %get-tuple-element.58, bf16[2,2,1,240,320]{4,3,1,0,2:T(8,128)(2,1)} %get-tuple-element.59), kind=kLoop, calls=%fused_computation.10 | loop fusion | flops 614400 | bytes 2457600 | tf_op jit(solution)/shard_map/stack | solution.py:58
  66.1 1.7 %copy.282 = bf16[2,2,2,240,320]{3,4,2,1,0:T(8,128)(2,1)S(1)} copy(bf16[2,2,2,240,320]{4,3,1,0,2:T(8,128)(2,1)} %pad_maximum_fusion) | data formatting | bytes 2457600 | tf_op jit(solution)/shard_map/stack | solution.py:58
  70.6 2.2 %fusion.110 = f32[512,1280]{1,0:T(8,128)S(1)} fusion(bf16[1280,320]{1,0:T(8,128)(2,1)} %bitcast.170, f32[512,320]{0,1:T(8,128)S(1)} %get-tuple-element.23, f32[320]{0:T(512)S(1)} %copy-done.18, f32[320]{0:T(512)S(1)} %copy-done.17, f32[512]{0:T(512)S(1)} %add_rsqrt_fusion.1, f32[512]{0:T(512)S(1)} %broadcast_multiply_fusion.3), kind=kOutput, calls=%fused_computation.217 | convolution fusion | flops 420249600 | bytes 4102656 | tf_op jit(solution)/shard_map/dot_general | solution.py:28
  80.7 2.4 %reshape.158 = f32[2,256,320]{1,0,2:T(2,128)} reshape(f32[512,320]{0,1:T(8,128)} %multiply_add_fusion.2) | data formatting | bytes 1310720 | tf_op jit(solution)/shard_map/reshape | solution.py:225
  86.4 2.3 %collective-permute-start.26 = (f32[4,320]{0,1:T(8,128)}, f32[4,320]{0,1:T(8,128)}, u32[]{:S(2)}, u32[]{:S(2)}) collective-permute-start(f32[4,320]{0,1:T(8,128)} %pad_maximum_fusion.11), channel_id=1, source_target_pairs={{0,24},{4,28},{8,16},{12,20},{16,8},{20,12},{24,0},{28,4},{1,25},{... | collective-permute-start | bytes 15368 | tf_op jit(solution)/shard_map/ppermute | solution.py:47
  92.7 2.3 %fusion.26 = f32[4,2,160,320]{3,2,1,0:T(8,128)S(1)} fusion(bf16[4,2,160,512]{3,2,1,0:T(8,128)(2,1)} %bitcast.169, f32[512,320]{0,1:T(8,128)S(1)} %get-tuple-element.23, f32[320]{0:T(512)S(1)} %copy-done.18, f32[320]{0:T(512)S(1)} %copy-done.17, f32[512]{0:T(512)S(1)} %add_rsqrt_fusion.1, f32[512]{0:T(512)S(1)} %broadcast_multiply_fusion.3), kind=kOutput, calls=%fused_computation.65 | convolution fusion | flops 420249600 | bytes 3611136 | tf_op jit(solution)/shard_map/dot_general | solution.py:34
  98.8 2.2 %collective-permute-start.25 = (f32[4,320]{0,1:T(8,128)}, f32[4,320]{0,1:T(8,128)}, u32[]{:S(2)}, u32[]{:S(2)}) collective-permute-start(f32[4,320]{0,1:T(8,128)} %pad_maximum_fusion.11), channel_id=1, source_target_pairs={{0,20},{4,16},{8,28},{12,24},{16,4},{20,0},{24,12},{28,8},{1,21},{... | collective-permute-start | bytes 15368 | tf_op jit(solution)/shard_map/ppermute | solution.py:47
  104.5 1.7 %slice.217 = f32[2,320]{0,1:T(8,128)} slice(f32[4,320]{0,1:T(8,128)} %collective-permute-done.22), slice={[2:4], [0:320]} | slice | bytes 5120 | tf_op jit(solution)/shard_map/slice | solution.py:240
  107.2 1.7 %slice.216 = f32[2,320]{0,1:T(8,128)} slice(f32[4,320]{0,1:T(8,128)} %collective-permute-done.21), slice={[2:4], [0:320]} | slice | bytes 5120 | tf_op jit(solution)/shard_map/slice | solution.py:240
  110.8 2.1 %fusion.38 = f32[2,320]{0,1:T(8,128)} fusion(f32[2,320]{0,1:T(8,128)} %copy.305, f32[4,320]{0,1:T(8,128)} %collective-permute-done.27, f32[4,320]{0,1:T(8,128)} %collective-permute-done.26, f32[4,320]{0,1:T(8,128)} %collective-permute-done.25, f32[4,320]{0,1:T(8,128)} %collective-permute-done.24), kind=kLoop, calls=%fused_computation.91 | loop fusion | flops 2560 | bytes 15360 | tf_op jit(solution)/shard_map/add | solution.py:42
  112.9 3.6 %collective-permute-start.36 = (f32[2,320]{0,1:T(8,128)}, f32[2,320]{0,1:T(8,128)}, u32[]{:S(2)}, u32[]{:S(2)}) collective-permute-start(f32[2,320]{0,1:T(8,128)} %fusion.38), channel_id=1, source_target_pairs={{0,3},{1,2},{2,1},{3,0},{4,7},{5,6},{6,5},{7,4},{8,11},{9,10},{10,... | collective-permute-start | bytes 7688 | tf_op jit(solution)/shard_map/ppermute | solution.py:47
  128.7 2.7 %collective-permute-done.35 = f32[2,320]{0,1:T(8,128)} collective-permute-done((f32[2,320]{0,1:T(8,128)}, f32[2,320]{0,1:T(8,128)}, u32[]{:S(2)}, u32[]{:S(2)}) %collective-permute-start.35) | collective-permute-done | bytes 2592 | tf_op jit(solution)/shard_map/ppermute | solution.py:47
  132.9 1.8 %collective-permute-done.20 = bf16[240,320]{0,1:T(8,128)(2,1)S(1)} collective-permute-done((bf16[240,320]{0,1:T(8,128)(2,1)S(1)}, bf16[240,320]{0,1:T(8,128)(2,1)S(1)}, u32[]{:S(2)}, u32[]{:S(2)}) %collective-permute-start.20) | collective-permute-done | bytes 153632 | tf_op jit(solution)/shard_map/ppermute | solution.py:47
  136.7 1.7 %collective-permute-start.28 = (bf16[80,320]{1,0:T(8,128)(2,1)S(1)}, bf16[80,320]{1,0:T(8,128)(2,1)S(1)}, u32[]{:S(2)}, u32[]{:S(2)}) collective-permute-start(bf16[80,320]{1,0:T(8,128)(2,1)S(1)} %get-tuple-element.39), channel_id=1, source_target_pairs={{0,1},{1,0},{2,3},{3,2},{4,5},{5,4},{6,7},{7,6},{8,9},{9,8},{10,11... | collective-permute-start | bytes 153608 | tf_op jit(solution)/shard_map/ppermute | solution.py:47
  138.3 2.5 %collective-permute-start.30 = (bf16[80,320]{1,0:T(8,128)(2,1)S(1)}, bf16[80,320]{1,0:T(8,128)(2,1)S(1)}, u32[]{:S(2)}, u32[]{:S(2)}) collective-permute-start(bf16[80,320]{1,0:T(8,128)(2,1)S(1)} %get-tuple-element.40), channel_id=1, source_target_pairs={{0,3},{1,2},{2,1},{3,0},{4,7},{5,6},{6,5},{7,4},{8,11},{9,10},{10,... | collective-permute-start | bytes 153608 | tf_op jit(solution)/shard_map/ppermute | solution.py:47
  141.4 3.0 %collective-permute-done.30 = bf16[80,320]{1,0:T(8,128)(2,1)S(1)} collective-permute-done((bf16[80,320]{1,0:T(8,128)(2,1)S(1)}, bf16[80,320]{1,0:T(8,128)(2,1)S(1)}, u32[]{:S(2)}, u32[]{:S(2)}) %collective-permute-start.30) | collective-permute-done | bytes 51232 | tf_op jit(solution)/shard_map/ppermute | solution.py:47
  144.4 2.2 %collective-permute-done.29 = bf16[80,320]{1,0:T(8,128)(2,1)S(1)} collective-permute-done((bf16[80,320]{1,0:T(8,128)(2,1)S(1)}, bf16[80,320]{1,0:T(8,128)(2,1)S(1)}, u32[]{:S(2)}, u32[]{:S(2)}) %collective-permute-start.29) | collective-permute-done | bytes 51232 | tf_op jit(solution)/shard_map/ppermute | solution.py:47
  147.3 2.4 %collective-permute-start.32 = (bf16[80,320]{1,0:T(8,128)(2,1)S(1)}, bf16[80,320]{1,0:T(8,128)(2,1)S(1)}, u32[]{:S(2)}, u32[]{:S(2)}) collective-permute-start(bf16[80,320]{1,0:T(8,128)(2,1)S(1)} %get-tuple-element.21), channel_id=1, source_target_pairs={{0,2},{1,3},{2,0},{3,1},{4,6},{5,7},{6,4},{7,5},{8,10},{9,11},{10,... | collective-permute-start | bytes 153608 | tf_op jit(solution)/shard_map/ppermute | solution.py:47
  149.8 1.9 %collective-permute-start.33 = (bf16[80,320]{1,0:T(8,128)(2,1)S(1)}, bf16[80,320]{1,0:T(8,128)(2,1)S(1)}, u32[]{:S(2)}, u32[]{:S(2)}) collective-permute-start(bf16[80,320]{1,0:T(8,128)(2,1)S(1)} %get-tuple-element.21), channel_id=1, source_target_pairs={{0,3},{1,2},{2,1},{3,0},{4,7},{5,6},{6,5},{7,4},{8,11},{9,10},{10,... | collective-permute-start | bytes 153608 | tf_op jit(solution)/shard_map/ppermute | solution.py:47
  152.8 3.0 %collective-permute-done.33 = bf16[80,320]{1,0:T(8,128)(2,1)S(1)} collective-permute-done((bf16[80,320]{1,0:T(8,128)(2,1)S(1)}, bf16[80,320]{1,0:T(8,128)(2,1)S(1)}, u32[]{:S(2)}, u32[]{:S(2)}) %collective-permute-start.33) | collective-permute-done | bytes 51232 | tf_op jit(solution)/shard_map/ppermute | solution.py:47
  (228 shorter events, 79.4 us)
Async XLA Ops:
  0.7 7.7 %collective-permute-start.4 = (s32[2]{0:T(128)}, s32[2]{0:T(128)S(1)}, u32[]{:S(2)}, u32[]{:S(2)}) collective-permute-start(s32[2]{0:T(128)} %param.15), channel_id=1, source_target_pairs={{0,20},{4,16},{8,28},{12,24},{16,4},{20,0},{24,12},{28,8},{1,21},{... | collective-permute-start | bytes 32 | tf_op jit(solution)/shard_map/ppermute | solution.py:47
  3.2 7.9 %collective-permute-start.3 = (s32[2]{0:T(128)}, s32[2]{0:T(128)S(1)}, u32[]{:S(2)}, u32[]{:S(2)}) collective-permute-start(s32[2]{0:T(128)} %param.15), channel_id=1, source_target_pairs={{0,16},{4,20},{8,24},{12,28},{16,0},{20,4},{24,8},{28,12},{1,17},{... | collective-permute-start | bytes 32 | tf_op jit(solution)/shard_map/ppermute | solution.py:47
  3.8 7.6 %collective-permute-start.2 = (s32[2]{0:T(128)}, s32[2]{0:T(128)S(1)}, u32[]{:S(2)}, u32[]{:S(2)}) collective-permute-start(s32[2]{0:T(128)} %param.15), channel_id=1, source_target_pairs={{0,12},{4,8},{8,4},{12,0},{16,28},{20,24},{24,20},{28,16},{1,13},{... | collective-permute-start | bytes 32 | tf_op jit(solution)/shard_map/ppermute | solution.py:47
  5.2 6.4 %collective-permute-start.1 = (s32[2]{0:T(128)}, s32[2]{0:T(128)S(1)}, u32[]{:S(2)}, u32[]{:S(2)}) collective-permute-start(s32[2]{0:T(128)} %param.15), channel_id=1, source_target_pairs={{0,8},{4,12},{8,0},{12,4},{16,24},{20,28},{24,16},{28,20},{1,9},{5... | collective-permute-start | bytes 32 | tf_op jit(solution)/shard_map/ppermute | solution.py:47
  5.5 6.2 %collective-permute-start = (s32[2]{0:T(128)}, s32[2]{0:T(128)S(1)}, u32[]{:S(2)}, u32[]{:S(2)}) collective-permute-start(s32[2]{0:T(128)} %param.15), channel_id=1, source_target_pairs={{0,4},{4,0},{8,12},{12,8},{16,20},{20,16},{24,28},{28,24},{1,5},{5... | collective-permute-start | bytes 32 | tf_op jit(solution)/shard_map/ppermute | solution.py:47
  19.4 13.7 %collective-permute-start.11 = (bf16[240,320]{1,0:T(8,128)(2,1)}, bf16[240,320]{1,0:T(8,128)(2,1)}, u32[]{:S(2)}, u32[]{:S(2)}) collective-permute-start(bf16[240,320]{1,0:T(8,128)(2,1)} %pad_maximum_fusion.9), channel_id=1, source_target_pairs={{0,8},{4,12},{8,0},{12,4},{16,24},{20,28},{24,16},{28,20},{1,9},{5... | collective-permute-start | bytes 460808 | tf_op jit(solution)/shard_map/ppermute | solution.py:47
  20.0 6.9 %collective-permute-start.10 = (f32[4,320]{1,0:T(4,128)S(1)}, f32[4,320]{1,0:T(4,128)S(1)}, u32[]{:S(2)}, u32[]{:S(2)}) collective-permute-start(f32[4,320]{1,0:T(4,128)S(1)} %get-tuple-element.46), channel_id=1, source_target_pairs={{0,24},{4,28},{8,16},{12,20},{16,8},{20,12},{24,0},{28,4},{1,25},{... | collective-permute-start | bytes 15368 | tf_op jit(solution)/shard_map/ppermute | solution.py:47
  21.5 5.4 %collective-permute-start.9 = (f32[4,320]{1,0:T(4,128)S(1)}, f32[4,320]{1,0:T(4,128)S(1)}, u32[]{:S(2)}, u32[]{:S(2)}) collective-permute-start(f32[4,320]{1,0:T(4,128)S(1)} %get-tuple-element.47), channel_id=1, source_target_pairs={{0,16},{4,20},{8,24},{12,28},{16,0},{20,4},{24,8},{28,12},{1,17},{... | collective-permute-start | bytes 15368 | tf_op jit(solution)/shard_map/ppermute | solution.py:47
  24.3 6.3 %collective-permute-start.14 = (bf16[240,320]{1,0:T(8,128)(2,1)}, bf16[240,320]{1,0:T(8,128)(2,1)}, u32[]{:S(2)}, u32[]{:S(2)}) collective-permute-start(bf16[240,320]{1,0:T(8,128)(2,1)} %pad_maximum_fusion.10), channel_id=1, source_target_pairs={{0,16},{4,20},{8,24},{12,28},{16,0},{20,4},{24,8},{28,12},{1,17},{... | collective-permute-start | bytes 460808 | tf_op jit(solution)/shard_map/ppermute | solution.py:47
  31.6 9.1 %collective-permute-start.15 = (bf16[2,240,320]{2,1,0:T(8,128)(2,1)S(1)}, bf16[2,240,320]{2,1,0:T(8,128)(2,1)S(1)}, u32[]{:S(2)}, u32[]{:S(2)}) collective-permute-start(bf16[2,240,320]{2,1,0:T(8,128)(2,1)S(1)} %pad_maximum_fusion.8), channel_id=1, source_target_pairs={{0,8},{4,12},{8,0},{12,4},{16,24},{20,28},{24,16},{28,20},{1,9},{5... | collective-permute-start | bytes 921608 | tf_op jit(solution)/shard_map/ppermute | solution.py:47
  34.9 9.0 %collective-permute-start.12 = (bf16[2,240,320]{2,1,0:T(8,128)(2,1)}, bf16[2,240,320]{2,1,0:T(8,128)(2,1)}, u32[]{:S(2)}, u32[]{:S(2)}) collective-permute-start(bf16[2,240,320]{2,1,0:T(8,128)(2,1)} %pad_maximum_fusion.7), channel_id=1, source_target_pairs={{0,16},{4,20},{8,24},{12,28},{16,0},{20,4},{24,8},{28,12},{1,17},{... | collective-permute-start | bytes 921608 | tf_op jit(solution)/shard_map/ppermute | solution.py:47
  42.2 6.5 %collective-permute-start.16 = (bf16[2,2,240,320]{2,3,1,0:T(8,128)(2,1)}, bf16[2,2,240,320]{2,3,1,0:T(8,128)(2,1)}, u32[]{:S(2)}, u32[]{:S(2)}) collective-permute-start(bf16[2,2,240,320]{2,3,1,0:T(8,128)(2,1)} %copy.287), channel_id=1, source_target_pairs={{0,4},{4,0},{8,12},{12,8},{16,20},{20,16},{24,28},{28,24},{1,5},{5... | collective-permute-start | bytes 1843208 | tf_op jit(solution)/shard_map/ppermute | solution.py:47
  85.6 25.1 %collective-permute-start.27 = (f32[4,320]{0,1:T(8,128)}, f32[4,320]{0,1:T(8,128)}, u32[]{:S(2)}, u32[]{:S(2)}) collective-permute-start(f32[4,320]{0,1:T(8,128)} %pad_maximum_fusion.11), channel_id=1, source_target_pairs={{0,28},{4,24},{8,20},{12,16},{16,12},{20,8},{24,4},{28,0},{1,29},{... | collective-permute-start | bytes 15368 | tf_op jit(solution)/shard_map/ppermute | solution.py:47
  86.4 24.4 %collective-permute-start.26 = (f32[4,320]{0,1:T(8,128)}, f32[4,320]{0,1:T(8,128)}, u32[]{:S(2)}, u32[]{:S(2)}) collective-permute-start(f32[4,320]{0,1:T(8,128)} %pad_maximum_fusion.11), channel_id=1, source_target_pairs={{0,24},{4,28},{8,16},{12,20},{16,8},{20,12},{24,0},{28,4},{1,25},{... | collective-permute-start | bytes 15368 | tf_op jit(solution)/shard_map/ppermute | solution.py:47
  88.7 10.1 %collective-permute-start.23 = (f32[4,320]{0,1:T(8,128)}, f32[4,320]{0,1:T(8,128)S(1)}, u32[]{:S(2)}, u32[]{:S(2)}) collective-permute-start(f32[4,320]{0,1:T(8,128)} %pad_maximum_fusion.11), channel_id=1, source_target_pairs={{0,12},{4,8},{8,4},{12,0},{16,28},{20,24},{24,20},{28,16},{1,13},{... | collective-permute-start | bytes 15368 | tf_op jit(solution)/shard_map/ppermute | solution.py:47
  88.7 14.4 %collective-permute-start.22 = (f32[4,320]{0,1:T(8,128)}, f32[4,320]{0,1:T(8,128)}, u32[]{:S(2)}, u32[]{:S(2)}) collective-permute-start(f32[4,320]{0,1:T(8,128)} %pad_maximum_fusion.11), channel_id=1, source_target_pairs={{0,8},{4,12},{8,0},{12,4},{16,24},{20,28},{24,16},{28,20},{1,9},{5... | collective-permute-start | bytes 15368 | tf_op jit(solution)/shard_map/ppermute | solution.py:47
  90.0 17.1 %collective-permute-start.21 = (f32[4,320]{0,1:T(8,128)}, f32[4,320]{0,1:T(8,128)}, u32[]{:S(2)}, u32[]{:S(2)}) collective-permute-start(f32[4,320]{0,1:T(8,128)} %pad_maximum_fusion.11), channel_id=1, source_target_pairs={{0,4},{4,0},{8,12},{12,8},{16,20},{20,16},{24,28},{28,24},{1,5},{5... | collective-permute-start | bytes 15368 | tf_op jit(solution)/shard_map/ppermute | solution.py:47
  98.8 12.0 %collective-permute-start.25 = (f32[4,320]{0,1:T(8,128)}, f32[4,320]{0,1:T(8,128)}, u32[]{:S(2)}, u32[]{:S(2)}) collective-permute-start(f32[4,320]{0,1:T(8,128)} %pad_maximum_fusion.11), channel_id=1, source_target_pairs={{0,20},{4,16},{8,28},{12,24},{16,4},{20,0},{24,12},{28,8},{1,21},{... | collective-permute-start | bytes 15368 | tf_op jit(solution)/shard_map/ppermute | solution.py:47
  103.1 7.7 %collective-permute-start.24 = (f32[4,320]{0,1:T(8,128)}, f32[4,320]{0,1:T(8,128)}, u32[]{:S(2)}, u32[]{:S(2)}) collective-permute-start(f32[4,320]{0,1:T(8,128)} %pad_maximum_fusion.11), channel_id=1, source_target_pairs={{0,16},{4,20},{8,24},{12,28},{16,0},{20,4},{24,8},{28,12},{1,17},{... | collective-permute-start | bytes 15368 | tf_op jit(solution)/shard_map/ppermute | solution.py:47
  107.2 16.7 %collective-permute-start.17 = (bf16[4,240,320]{1,2,0:T(8,128)(2,1)S(1)}, bf16[4,240,320]{1,2,0:T(8,128)(2,1)}, u32[]{:S(2)}, u32[]{:S(2)}) collective-permute-start(bf16[4,240,320]{1,2,0:T(8,128)(2,1)S(1)} %copy.296), channel_id=1, source_target_pairs={{0,4},{4,0},{8,12},{12,8},{16,20},{20,16},{24,28},{28,24},{1,5},{5... | collective-permute-start | bytes 1843208 | tf_op jit(solution)/shard_map/ppermute | solution.py:47
  112.9 14.4 %collective-permute-start.36 = (f32[2,320]{0,1:T(8,128)}, f32[2,320]{0,1:T(8,128)}, u32[]{:S(2)}, u32[]{:S(2)}) collective-permute-start(f32[2,320]{0,1:T(8,128)} %fusion.38), channel_id=1, source_target_pairs={{0,3},{1,2},{2,1},{3,0},{4,7},{5,6},{6,5},{7,4},{8,11},{9,10},{10,... | collective-permute-start | bytes 7688 | tf_op jit(solution)/shard_map/ppermute | solution.py:47
  116.5 14.9 %collective-permute-start.35 = (f32[2,320]{0,1:T(8,128)}, f32[2,320]{0,1:T(8,128)}, u32[]{:S(2)}, u32[]{:S(2)}) collective-permute-start(f32[2,320]{0,1:T(8,128)} %fusion.38), channel_id=1, source_target_pairs={{0,2},{1,3},{2,0},{3,1},{4,6},{5,7},{6,4},{7,5},{8,10},{9,11},{10,... | collective-permute-start | bytes 7688 | tf_op jit(solution)/shard_map/ppermute | solution.py:47
  116.6 14.9 %collective-permute-start.34 = (f32[2,320]{0,1:T(8,128)}, f32[2,320]{0,1:T(8,128)}, u32[]{:S(2)}, u32[]{:S(2)}) collective-permute-start(f32[2,320]{0,1:T(8,128)} %fusion.38), channel_id=1, source_target_pairs={{0,1},{1,0},{2,3},{3,2},{4,5},{5,4},{6,7},{7,6},{8,9},{9,8},{10,11... | collective-permute-start | bytes 7688 | tf_op jit(solution)/shard_map/ppermute | solution.py:47
  125.2 7.7 %collective-permute-start.18 = (bf16[240,320]{0,1:T(8,128)(2,1)S(1)}, bf16[240,320]{0,1:T(8,128)(2,1)S(1)}, u32[]{:S(2)}, u32[]{:S(2)}) collective-permute-start(bf16[240,320]{0,1:T(8,128)(2,1)S(1)} %get-tuple-element.30), channel_id=1, source_target_pairs={{0,8},{4,12},{8,0},{12,4},{16,24},{20,28},{24,16},{28,20},{1,9},{5... | collective-permute-start | bytes 460808 | tf_op jit(solution)/shard_map/ppermute | solution.py:47
  125.9 8.8 %collective-permute-start.20 = (bf16[240,320]{0,1:T(8,128)(2,1)S(1)}, bf16[240,320]{0,1:T(8,128)(2,1)S(1)}, u32[]{:S(2)}, u32[]{:S(2)}) collective-permute-start(bf16[240,320]{0,1:T(8,128)(2,1)S(1)} %get-tuple-element.31), channel_id=1, source_target_pairs={{0,24},{4,28},{8,16},{12,20},{16,8},{20,12},{24,0},{28,4},{1,25},{... | collective-permute-start | bytes 460808 | tf_op jit(solution)/shard_map/ppermute | solution.py:47
  127.3 8.8 %collective-permute-start.19 = (bf16[240,320]{0,1:T(8,128)(2,1)S(1)}, bf16[240,320]{0,1:T(8,128)(2,1)S(1)}, u32[]{:S(2)}, u32[]{:S(2)}) collective-permute-start(bf16[240,320]{0,1:T(8,128)(2,1)S(1)} %get-tuple-element.32), channel_id=1, source_target_pairs={{0,16},{4,20},{8,24},{12,28},{16,0},{20,4},{24,8},{28,12},{1,17},{... | collective-permute-start | bytes 460808 | tf_op jit(solution)/shard_map/ppermute | solution.py:47
  136.7 4.8 %collective-permute-start.28 = (bf16[80,320]{1,0:T(8,128)(2,1)S(1)}, bf16[80,320]{1,0:T(8,128)(2,1)S(1)}, u32[]{:S(2)}, u32[]{:S(2)}) collective-permute-start(bf16[80,320]{1,0:T(8,128)(2,1)S(1)} %get-tuple-element.39), channel_id=1, source_target_pairs={{0,1},{1,0},{2,3},{3,2},{4,5},{5,4},{6,7},{7,6},{8,9},{9,8},{10,11... | collective-permute-start | bytes 153608 | tf_op jit(solution)/shard_map/ppermute | solution.py:47
  138.3 6.1 %collective-permute-start.30 = (bf16[80,320]{1,0:T(8,128)(2,1)S(1)}, bf16[80,320]{1,0:T(8,128)(2,1)S(1)}, u32[]{:S(2)}, u32[]{:S(2)}) collective-permute-start(bf16[80,320]{1,0:T(8,128)(2,1)S(1)} %get-tuple-element.40), channel_id=1, source_target_pairs={{0,3},{1,2},{2,1},{3,0},{4,7},{5,6},{6,5},{7,4},{8,11},{9,10},{10,... | collective-permute-start | bytes 153608 | tf_op jit(solution)/shard_map/ppermute | solution.py:47
  140.8 5.8 %collective-permute-start.29 = (bf16[80,320]{1,0:T(8,128)(2,1)S(1)}, bf16[80,320]{1,0:T(8,128)(2,1)S(1)}, u32[]{:S(2)}, u32[]{:S(2)}) collective-permute-start(bf16[80,320]{1,0:T(8,128)(2,1)S(1)} %get-tuple-element.41), channel_id=1, source_target_pairs={{0,2},{1,3},{2,0},{3,1},{4,6},{5,7},{6,4},{7,5},{8,10},{9,11},{10,... | collective-permute-start | bytes 153608 | tf_op jit(solution)/shard_map/ppermute | solution.py:47
  146.7 5.0 %collective-permute-start.31 = (bf16[80,320]{1,0:T(8,128)(2,1)S(1)}, bf16[80,320]{1,0:T(8,128)(2,1)S(1)}, u32[]{:S(2)}, u32[]{:S(2)}) collective-permute-start(bf16[80,320]{1,0:T(8,128)(2,1)S(1)} %get-tuple-element.21), channel_id=1, source_target_pairs={{0,1},{1,0},{2,3},{3,2},{4,5},{5,4},{6,7},{7,6},{8,9},{9,8},{10,11... | collective-permute-start | bytes 153608 | tf_op jit(solution)/shard_map/ppermute | solution.py:47
  147.3 5.4 %collective-permute-start.32 = (bf16[80,320]{1,0:T(8,128)(2,1)S(1)}, bf16[80,320]{1,0:T(8,128)(2,1)S(1)}, u32[]{:S(2)}, u32[]{:S(2)}) collective-permute-start(bf16[80,320]{1,0:T(8,128)(2,1)S(1)} %get-tuple-element.21), channel_id=1, source_target_pairs={{0,2},{1,3},{2,0},{3,1},{4,6},{5,7},{6,4},{7,5},{8,10},{9,11},{10,... | collective-permute-start | bytes 153608 | tf_op jit(solution)/shard_map/ppermute | solution.py:47
  149.8 6.0 %collective-permute-start.33 = (bf16[80,320]{1,0:T(8,128)(2,1)S(1)}, bf16[80,320]{1,0:T(8,128)(2,1)S(1)}, u32[]{:S(2)}, u32[]{:S(2)}) collective-permute-start(bf16[80,320]{1,0:T(8,128)(2,1)S(1)} %get-tuple-element.21), channel_id=1, source_target_pairs={{0,3},{1,2},{2,1},{3,0},{4,7},{5,6},{6,5},{7,4},{8,11},{9,10},{10,... | collective-permute-start | bytes 153608 | tf_op jit(solution)/shard_map/ppermute | solution.py:47
  (32 other events, 237.3 us)

commit v2 on v0

--- a/solution.py
+++ b/solution.py
@@ -3,6 +3,8 @@
 import jax
 import jax.numpy as jnp
 from jax import lax
+from jax.experimental import pallas as pl
+from jax.experimental.pallas import tpu as pltpu
 from jax.sharding import PartitionSpec as P
 
 SKIP = 20
@@ -170,6 +172,239 @@
     )
 
 
+def exchange(x, axis, count, mask):
+    return lax.ppermute(x, axis, [(i, i ^ mask) for i in range(count)])
+
+
+def gather_doubling(x, count, order):
+    masks = [0]
+    for bit in order[:-1]:
+        x = jnp.concatenate([x, exchange(x, "dp", count, 1 << bit)])
+        masks = masks + [m ^ (1 << bit) for m in masks]
+    return x, exchange(x, "dp", count, 1 << order[-1]), masks, 1 << order[-1]
+
+
+def sum_over_rep(x, count):
+    me = lax.axis_index("rep")
+    rows = x.shape[0] // count
+    chunk = lambda k: lax.dynamic_slice_in_dim(x, (me ^ k) * rows, rows, axis=0)
+    total = chunk(0)
+    for k in range(1, count):
+        total = total + exchange(chunk(k).astype(jnp.bfloat16), "rep", count, k).astype(jnp.float32)
+    total = total.astype(jnp.bfloat16)
+    out = jnp.zeros(x.shape, jnp.float32)
+    for k in range(count):
+        got = exchange(total, "rep", count, k) if k else total
+        out = lax.dynamic_update_slice_in_dim(out, got.astype(jnp.float32), (me ^ k) * rows, axis=0)
+    return out
+
+
+def step_kernel(sizes, s_masks, s_far, t_masks, t_far):
+    count, in_rows, out_rows, time_rows, samples, tokens, width = sizes
+    rows = in_rows + out_rows + time_rows
+    hidden_count = out_rows * count
+
+    def body(
+        me_ref, s_tok, t_tok, s_feat, t_feat, s_feat_t, s_gain, s_bias, t_gain, t_bias,
+        s_near_ref, s_far_ref, t_near_ref, t_far_ref,
+        away_ref, keep_ref, affine_ref,
+        sw_in, sw_out, sw_time, tw_in, tw_out, tw_time, g_in, g_out, g_time, s_emb, t_emb, emb_grad,
+    ):
+        me = me_ref[0]
+
+        def place(ref, masks, flip, w_in, w_out, w_time):
+            for p, mask in enumerate(masks):
+                at = me ^ (mask ^ flip)
+                base = p * rows
+                w_in[pl.ds(pl.multiple_of(at * in_rows, 16), in_rows), :] = ref[base : base + in_rows, :]
+                base = base + in_rows
+                w_out[pl.ds(pl.multiple_of(at * out_rows, 16), out_rows), :] = ref[base : base + out_rows, :]
+                base = base + out_rows
+                w_time[pl.ds(pl.multiple_of(at * time_rows, 16), time_rows), :] = ref[base : base + time_rows, :]
+
+        place(s_near_ref, s_masks, 0, sw_in, sw_out, sw_time)
+        place(s_far_ref, s_masks, s_far, sw_in, sw_out, sw_time)
+        place(t_near_ref, t_masks, 0, tw_in, tw_out, tw_time)
+        place(t_far_ref, t_masks, t_far, tw_in, tw_out, tw_time)
+        s_emb[...] = jnp.dot(s_feat[...], sw_time[...], preferred_element_type=jnp.float32)
+        t_emb[...] = jnp.dot(t_feat[...], tw_time[...], preferred_element_type=jnp.float32)
+        g_in[...] = jnp.zeros_like(g_in)
+        g_out[...] = jnp.zeros_like(g_out)
+        affine_ref[...] = jnp.zeros_like(affine_ref)
+
+        def norm(tok, emb, gain, bias):
+            summed = tok.astype(jnp.float32) + emb
+            center = summed - jnp.mean(summed, axis=1, keepdims=True)
+            inv_std = lax.rsqrt(jnp.mean(center * center, axis=1, keepdims=True) + 1e-05)
+            normed = center * inv_std
+            return summed, normed, inv_std, (normed * gain + bias).astype(jnp.bfloat16)
+
+        for s in range(samples):
+            at = slice(s * tokens, (s + 1) * tokens)
+            t_sum, _, _, t_norm = norm(t_tok[at, :], t_emb[s : s + 1, :], t_gain[...], t_bias[...])
+            t_mixed = contract_last(t_norm, tw_in[...])
+            t_hidden = (gelu_tanh(t_mixed[:, :hidden_count]) * t_mixed[:, hidden_count:]).astype(jnp.bfloat16)
+            t_res = t_sum + jnp.dot(t_hidden, tw_out[...], preferred_element_type=jnp.float32)
+            s_sum, normed, inv_std, normed_b = norm(s_tok[at, :], s_emb[s : s + 1, :], s_gain[...], s_bias[...])
+            mixed = contract_last(normed_b, sw_in[...])
+            gate = mixed[:, :hidden_count]
+            up = mixed[:, hidden_count:]
+            tangent = jnp.tanh(0.7978845608 * (gate + 0.044715 * gate * gate * gate))
+            gelu_gate = 0.5 * gate * (1.0 + tangent)
+            slope = 0.5 * (1.0 + tangent) + 0.5 * gate * (1.0 - tangent * tangent) * 0.7978845608 * (
+                1.0 + 0.134145 * gate * gate
+            )
+            hidden = (gelu_gate * up).astype(jnp.bfloat16)
+            s_res = s_sum + jnp.dot(hidden, sw_out[...], preferred_element_type=jnp.float32)
+            grad_y = (s_res - t_res) / (samples * tokens)
+            grad_yb = grad_y.astype(jnp.bfloat16)
+            g_out[...] += contract_first(hidden, grad_yb)
+            grad_h = contract_last(grad_yb, sw_out[...])
+            mix_gate = (grad_h * up * slope).astype(jnp.bfloat16)
+            mix_up = (grad_h * gelu_gate).astype(jnp.bfloat16)
+            g_in[:hidden_count, :] += contract_first(mix_gate, normed_b)
+            g_in[hidden_count:, :] += contract_first(mix_up, normed_b)
+            grad_z = jnp.dot(mix_gate, sw_in[:hidden_count, :], preferred_element_type=jnp.float32) + jnp.dot(
+                mix_up, sw_in[hidden_count:, :], preferred_element_type=jnp.float32
+            )
+            affine_ref[0:1, :] += jnp.sum(grad_z * normed, axis=0, keepdims=True)
+            affine_ref[1:2, :] += jnp.sum(grad_z, axis=0, keepdims=True)
+            grad_n = grad_z * s_gain[...]
+            grad_s = grad_y + inv_std * (
+                grad_n
+                - jnp.mean(grad_n, axis=1, keepdims=True)
+                - normed * jnp.mean(grad_n * normed, axis=1, keepdims=True)
+            )
+            emb_grad[s : s + 1, :] = jnp.sum(grad_s, axis=0, keepdims=True)
+
+        total = s_feat_t[:, 0:1] * emb_grad[0:1, :]
+        for s in range(1, samples):
+            total = total + s_feat_t[:, s : s + 1] * emb_grad[s : s + 1, :]
+        g_time[...] = total
+
+        for p in range(count // 2):
+            for flip, out in ((0, keep_ref), (1, away_ref)):
+                at = me ^ (2 * p + flip)
+                base = p * rows
+                for ref, size in ((g_in, in_rows), (g_out, out_rows), (g_time, time_rows)):
+                    out[base : base + size, :] = ref[pl.ds(pl.multiple_of(at * size, 16), size), :].astype(out.dtype)
+                    base = base + size
+
+    vm = pl.BlockSpec(memory_space=pltpu.VMEM)
+    f32, bf16 = jnp.float32, jnp.bfloat16
+    half = count // 2 * rows
+    return pl.pallas_call(
+        body,
+        in_specs=[pl.BlockSpec(memory_space=pltpu.SMEM)] + [vm] * 13,
+        out_specs=[vm] * 3,
+        out_shape=[
+            jax.ShapeDtypeStruct((half, width), bf16),
+            jax.ShapeDtypeStruct((half, width), f32),
+            jax.ShapeDtypeStruct((8, width), f32),
+        ],
+        scratch_shapes=[
+            pltpu.VMEM((in_rows * count, width), bf16),
+            pltpu.VMEM((out_rows * count, width), bf16),
+            pltpu.VMEM((time_rows * count, width), bf16),
+            pltpu.VMEM((in_rows * count, width), bf16),
+            pltpu.VMEM((out_rows * count, width), bf16),
+            pltpu.VMEM((time_rows * count, width), bf16),
+            pltpu.VMEM((in_rows * count, width), f32),
+            pltpu.VMEM((out_rows * count, width), f32),
+            pltpu.VMEM((time_rows * count, width), f32),
+            pltpu.VMEM((16, width), f32),
+            pltpu.VMEM((16, width), f32),
+            pltpu.VMEM((8, width), f32),
+        ],
+        compiler_params=pltpu.CompilerParams(vmem_limit_bytes=48 * 1024 * 1024),
+        name="distill_step",
+    )
+
+
+def make_paired(n_dp, n_rep):
+    bits = n_dp.bit_length() - 1
+
+    def paired(
+        student_in,
+        target_in,
+        timesteps,
+        student_win,
+        student_wout,
+        student_wtime,
+        student_gain,
+        student_bias,
+        target_win,
+        target_wout,
+        target_wtime,
+        target_gain,
+        target_bias,
+    ):
+        width = student_in.shape[1]
+        samples = timesteps.shape[0]
+        in_rows, out_rows, time_rows = student_win.shape[0], student_wout.shape[0], student_wtime.shape[0]
+        rows = in_rows + out_rows + time_rows
+        up = list(range(1, bits)) + [0]
+        down = list(range(bits - 1, 0, -1)) + [0]
+
+        def net(win, wout, wtime, order):
+            block = jnp.concatenate([win, wout, wtime]).astype(jnp.bfloat16)
+            return gather_doubling(block, n_dp, order)
+
+        s_near, s_far, s_masks, s_flip = net(student_win, student_wout, student_wtime, up)
+        t_near, t_far, t_masks, t_flip = net(target_win, target_wout, target_wtime, down)
+
+        def feats(ids):
+            feat = jax.nn.silu(sinusoid(ids, time_rows * n_dp)).astype(jnp.bfloat16)
+            return jnp.pad(feat, ((0, 16 - samples), (0, 0)))
+
+        s_feat = feats(timesteps)
+        t_feat = feats(timesteps - SKIP)
+        kernel = step_kernel(
+            (n_dp, in_rows, out_rows, time_rows, samples, student_in.shape[0] // samples, width),
+            s_masks, s_flip, t_masks, t_flip,
+        )
+        away, keep, affine = kernel(
+            lax.axis_index("dp").reshape(1),
+            student_in, target_in, s_feat, t_feat, s_feat.astype(jnp.float32).T,
+            student_gain[None], student_bias[None], target_gain[None], target_bias[None],
+            s_near, s_far, t_near, t_far,
+        )
+        near = exchange(away, "dp", n_dp, 1)
+        total = keep[:rows] + near[:rows].astype(jnp.float32)
+        for k in range(1, n_dp // 2):
+            at = slice(k * rows, (k + 1) * rows)
+            part = (keep[at] + near[at].astype(jnp.float32)).astype(jnp.bfloat16)
+            total = total + exchange(part, "dp", n_dp, 2 * k).astype(jnp.float32)
+        affine = affine[:2]
+        for bit in range(bits):
+            affine = affine + exchange(affine, "dp", n_dp, 1 << bit)
+        for bit in range(n_rep.bit_length() - 1):
+            affine = affine + exchange(affine, "rep", n_rep, 1 << bit)
+        total_gain, total_bias = affine[0], affine[1]
+        total = sum_over_rep(total, n_rep)
+        shard_in = total[:in_rows]
+        shard_out = total[in_rows : in_rows + out_rows]
+        shard_time = total[in_rows + out_rows :]
+
+        def average(target_p, student_p, grad_p):
+            return ema_decay * target_p + (1.0 - ema_decay) * (student_p - learn_rate * grad_p)
+
+        return (
+            shard_in,
+            shard_out,
+            shard_time,
+            total_gain,
+            total_bias,
+            average(target_win, student_win, shard_in),
+            average(target_wout, student_wout, shard_out),
+            average(target_wtime, student_wtime, shard_time),
+            average(target_gain, student_gain, total_gain),
+            average(target_bias, student_bias, total_bias),
+        )
+
+    return paired
+
+
 def solution(mesh):
     in_specs = (
         P(("dp", "rep"), None),
@@ -198,6 +433,8 @@
         P(),
         P(),
     )
+    n_dp, n_rep = mesh.shape["dp"], mesh.shape["rep"]
+    body = make_paired(n_dp, n_rep) if n_dp <= 8 else per_device
     return jax.shard_map(
-        per_device, mesh=mesh, in_specs=in_specs, out_specs=out_specs, check_vma=False
-    )
+        body, mesh=mesh, in_specs=in_specs, out_specs=out_specs, check_vma=False
+    )

time: 257 us -> 110 us (0.43)
  blocking collectives: 100 us -> 0 us
  waiting for transfers between devices: 110 us -> 42.3 us
  starting transfers between devices: 0.34 us -> 26.1 us
  local copies, waits for them, and re-layouts: 5.4 us -> 21.6 us
  between operations: 14.1 us -> 1.12 us
  matrix products: 12.8 us -> 0 us
  Pallas kernels: 0 us -> 8.35 us
  other arithmetic: 13.6 us -> 9.71 us
    reduce_scatter x3 -> x0, waiting for transfers between devices: 109 us -> none  [the longest x1 43.6 us: per_device(): lax.psum_scatter(contract_first(part, normed_b), 'dp', scatter_dimension=...]
    all_gather x6 -> x0, blocking collectives: 60.7 us -> none  [the longest x2 20.9 us: fetch(): lax.all_gather(piece_in, 'dp', axis=0, tiled=True)]
    ppermute x0 -> x21, waiting for transfers between devices: none -> 42.3 us  [exchange(): return lax.ppermute(x, axis, [(i, i ^ mask) for i in range(count)])]
    psum x1 -> x0, blocking collectives: 39.6 us -> none  [per_device(): total_gain, total_bias = lax.psum((grad_gain, grad_bias), ('dp', 'rep'))]
    ppermute x0 -> x21, starting transfers between devices: none -> 26.1 us  [exchange(): return lax.ppermute(x, axis, [(i, i ^ mask) for i in range(count)])]
    dot_general x11 -> x0, matrix products: 12.8 us -> none  [the longest x3 4.66 us: contract_last(): lax.dot_general(left, right, (((1,), (1,)), ((), ())), preferred_element_...]
    pallas_call x0 -> x1, Pallas kernels: none -> 8.35 us  [paired(): kernel(lax.axis_index('dp').reshape(1), student_in, target_in, s_feat, t_...]
    unnamed x57 -> x47, local copies, waits for them, and re-layouts: 4.17 us -> 11.1 us
  transfers between devices with their start and end apart: 4 -> 21, of which waited for: 4 -> 13; matrix products, arithmetic and copies ran while one was open for 4% -> 15% of each run, Pallas kernels for 0% -> 0%
where the time goes in v2:
time: 110 us; the launch traced here: 109 us
  waiting for transfers between devices  42.3 us (38%)
  starting transfers between devices  26.1 us (24%)
  local copies, waits for them, and re-layouts  21.6 us (20%)
  other arithmetic  9.71 us (9%)
  Pallas kernels  8.35 us (8%)
  between operations  1.12 us (1%)
    ppermute x21, waiting for transfers between devices, exchange(): return lax.ppermute(x, axis, [(i, i ^ mask) for i in range(count)])  42.3 us
    ppermute x21, starting transfers between devices, exchange(): return lax.ppermute(x, axis, [(i, i ^ mask) for i in range(count)])  26.1 us
    unnamed x47, local copies, waits for them, and re-layouts  11.1 us
    pallas_call x1, Pallas kernels, paired(): kernel(lax.axis_index('dp').reshape(1), student_in, target_in, s_feat, t_...  8.35 us
    unnamed x6, other arithmetic  3.88 us
    ppermute x2, local copies, waits for them, and re-layouts, exchange(): return lax.ppermute(x, axis, [(i, i ^ mask) for i in range(count)])  3.8 us
    concatenate x4, local copies, waits for them, and re-layouts, gather_doubling(): x = jnp.concatenate([x, exchange(x, 'dp', count, 1 << bit)])  3.07 us
    add x3, other arithmetic, average(): ema_decay * target_p + (1.0 - ema_decay) * (student_p - learn_rate * grad_p)  2.23 us
  transfers between devices with their start and end apart: 21, of which 13 were waited for; matrix products, arithmetic and copies ran while one was open for 15% of the time, Pallas kernels for 0%

profile of v2, /device:TPU:0, one launch (start us, length us, event | category | flops | bytes accessed | tf_op | source)
XLA Modules:
  0.0 109.1 jit_solution(3696494779984637748)
XLA Ops:
  3.6 3.1 %collective-permute-start.3 = (bf16[320,320]{1,0:T(8,128)(2,1)S(1)}, bf16[320,320]{1,0:T(8,128)(2,1)S(1)}, u32[]{:S(2)}, u32[]{:S(2)}) collective-permute-start(bf16[320,320]{1,0:T(8,128)(2,1)S(1)} %pad_maximum_fusion.3), channel_id=1, source_target_pairs={{0,16},{4,20},{8,24},{12,28},{16,0},{20,4},{24,8},{28,12},{1,17},{... | collective-permute-start | bytes 614408 | tf_op jit(solution)/shard_map/ppermute | solution.py:176
  7.7 1.6 %collective-permute-start = (bf16[320,320]{1,0:T(8,128)(2,1)S(1)}, bf16[320,320]{1,0:T(8,128)(2,1)S(1)}, u32[]{:S(2)}, u32[]{:S(2)}) collective-permute-start(bf16[320,320]{1,0:T(8,128)(2,1)S(1)} %pad_maximum_fusion.2), channel_id=1, source_target_pairs={{0,8},{4,12},{8,0},{12,4},{16,24},{20,28},{24,16},{28,20},{1,9},{5... | collective-permute-start | bytes 614408 | tf_op jit(solution)/shard_map/ppermute | solution.py:176
  9.3 3.3 %collective-permute-done.3 = bf16[320,320]{1,0:T(8,128)(2,1)S(1)} collective-permute-done((bf16[320,320]{1,0:T(8,128)(2,1)S(1)}, bf16[320,320]{1,0:T(8,128)(2,1)S(1)}, u32[]{:S(2)}, u32[]{:S(2)}) %collective-permute-start.3) | collective-permute-done | bytes 204832 | tf_op jit(solution)/shard_map/ppermute | solution.py:176
  12.6 1.8 %collective-permute-start.4 = (bf16[640,320]{1,0:T(8,128)(2,1)S(1)}, bf16[640,320]{1,0:T(8,128)(2,1)S(1)}, u32[]{:S(2)}, u32[]{:S(2)}) collective-permute-start(bf16[640,320]{1,0:T(8,128)(2,1)S(1)} %pad_maximum_fusion.1), channel_id=1, source_target_pairs={{0,8},{4,12},{8,0},{12,4},{16,24},{20,28},{24,16},{28,20},{1,9},{5... | collective-permute-start | bytes 1228808 | tf_op jit(solution)/shard_map/ppermute | solution.py:176
  14.4 1.4 %collective-permute-done = bf16[320,320]{1,0:T(8,128)(2,1)S(1)} collective-permute-done((bf16[320,320]{1,0:T(8,128)(2,1)S(1)}, bf16[320,320]{1,0:T(8,128)(2,1)S(1)}, u32[]{:S(2)}, u32[]{:S(2)}) %collective-permute-start) | collective-permute-done | bytes 204832 | tf_op jit(solution)/shard_map/ppermute | solution.py:176
  16.2 9.6 %collective-permute-done.4 = bf16[640,320]{1,0:T(8,128)(2,1)S(1)} collective-permute-done((bf16[640,320]{1,0:T(8,128)(2,1)S(1)}, bf16[640,320]{1,0:T(8,128)(2,1)S(1)}, u32[]{:S(2)}, u32[]{:S(2)}) %collective-permute-start.4) | collective-permute-done | bytes 409632 | tf_op jit(solution)/shard_map/ppermute | solution.py:176
  28.4 1.3 %copy.47 = bf16[1280,320]{0,1:T(8,128)(2,1)} copy(bf16[1280,320]{1,0:T(8,128)(2,1)S(1)} %constant_dynamic-update-slice_fusion.s_near_ref) | data formatting | bytes 1638400 | tf_op jit(solution)/shard_map/concatenate | solution.py:182
  30.5 1.2 %copy.49.s_tok = bf16[512,320]{1,0:T(8,128)(2,1)S(1)} copy(bf16[512,320]{0,1:T(8,128)(2,1)} %param.13) | data formatting | bytes 655360 | tf_op args[0]
  31.6 1.9 %copy.50.t_tok = bf16[512,320]{1,0:T(8,128)(2,1)} copy(bf16[512,320]{0,1:T(8,128)(2,1)} %param.14) | data formatting | bytes 655360 | tf_op args[1]
  34.4 1.5 %copy.53.t_far_ref = bf16[1280,320]{1,0:T(8,128)(2,1)S(1)} copy(bf16[1280,320]{0,1:T(8,128)(2,1)} %collective-permute-done.5) | data formatting | bytes 1638400 | tf_op jit(solution)/shard_map/ppermute | solution.py:176
  36.0 2.3 %copy.52.s_far_ref = bf16[1280,320]{1,0:T(8,128)(2,1)} copy(bf16[1280,320]{0,1:T(8,128)(2,1)} %collective-permute-done.2) | data formatting | bytes 1638400 | tf_op jit(solution)/shard_map/ppermute | solution.py:176
  38.2 1.2 %copy-done = bf16[1280,320]{1,0:T(8,128)(2,1)S(1)} copy-done((bf16[1280,320]{1,0:T(8,128)(2,1)S(1)}, bf16[1280,320]{1,0:T(8,128)(2,1)}, u32[]{:S(2)}) %copy-start) | copy-done | bytes 819224
  41.4 8.4 %distill_step.1 = (bf16[1280,320]{1,0:T(8,128)(2,1)S(1)}, f32[1280,320]{1,0:T(8,128)}, f32[8,320]{1,0:T(8,128)S(1)}) custom-call(s32[1]{0:T(128)} %bitcast.me_ref, bf16[512,320]{1,0:T(8,128)(2,1)S(1)} %copy.49.s_tok, bf16[512,320]{1,0:T(8,128)(2,1)S(1)} %copy-done.1, bf16[16,640]{1,0:T(8,128)(2,1)S(1)} %pad.7.clone.s_feat, bf16[16,640]{1,0:T(8,128)(2,1)S(1)} %pad.8.t_feat, ...), custom_call_target="tpu_custom_call" | custom-call | tf_op jit(solution)/shard_map/distill_step/pallas_call | solution.py:366
  50.7 2.2 %copy.54 = bf16[1280,320]{0,1:T(8,128)(2,1)} copy(bf16[1280,320]{1,0:T(8,128)(2,1)} %copy-done.3) | data formatting | bytes 1638400 | tf_op jit(solution)/shard_map/distill_step/pallas_call | solution.py:366
  53.5 2.1 %collective-permute-done.6 = bf16[1280,320]{0,1:T(8,128)(2,1)S(1)} collective-permute-done((bf16[1280,320]{0,1:T(8,128)(2,1)}, bf16[1280,320]{0,1:T(8,128)(2,1)S(1)}, u32[]{:S(2)}, u32[]{:S(2)}) %collective-permute-start.6) | collective-permute-done | bytes 819232 | tf_op jit(solution)/shard_map/ppermute | solution.py:176
  61.0 1.5 %collective-permute-start.7 = (bf16[320,320]{1,0:T(8,128)(2,1)}, bf16[320,320]{1,0:T(8,128)(2,1)S(1)}, u32[]{:S(2)}, u32[]{:S(2)}) collective-permute-start(bf16[320,320]{1,0:T(8,128)(2,1)} %get-tuple-element.38), channel_id=1, source_target_pairs={{0,8},{4,12},{8,0},{12,4},{16,24},{20,28},{24,16},{28,20},{1,9},{5... | collective-permute-start | bytes 614408 | tf_op jit(solution)/shard_map/ppermute | solution.py:176
  63.0 1.5 %collective-permute-start.9 = (bf16[320,320]{1,0:T(8,128)(2,1)}, bf16[320,320]{1,0:T(8,128)(2,1)}, u32[]{:S(2)}, u32[]{:S(2)}) collective-permute-start(bf16[320,320]{1,0:T(8,128)(2,1)} %get-tuple-element.39), channel_id=1, source_target_pairs={{0,24},{4,28},{8,16},{12,20},{16,8},{20,12},{24,0},{28,4},{1,25},{... | collective-permute-start | bytes 614408 | tf_op jit(solution)/shard_map/ppermute | solution.py:176
  64.5 1.5 %collective-permute-start.17 = (f32[2,320]{1,0:T(2,128)S(1)}, f32[2,320]{1,0:T(2,128)S(1)}, u32[]{:S(2)}, u32[]{:S(2)}) collective-permute-start(f32[2,320]{1,0:T(2,128)S(1)} %slice_add_fusion), channel_id=1, source_target_pairs={{0,8},{4,12},{8,0},{12,4},{16,24},{20,28},{24,16},{28,20},{1,9},{5... | collective-permute-start | bytes 7688 | tf_op jit(solution)/shard_map/ppermute | solution.py:176
  66.0 8.8 %collective-permute-done.17 = f32[2,320]{1,0:T(2,128)S(1)} collective-permute-done((f32[2,320]{1,0:T(2,128)S(1)}, f32[2,320]{1,0:T(2,128)S(1)}, u32[]{:S(2)}, u32[]{:S(2)}) %collective-permute-start.17) | collective-permute-done | bytes 2592 | tf_op jit(solution)/shard_map/ppermute | solution.py:176
  75.6 2.8 %collective-permute-done.18 = f32[2,320]{1,0:T(2,128)S(1)} collective-permute-done((f32[2,320]{1,0:T(2,128)S(1)}, f32[2,320]{1,0:T(2,128)S(1)}, u32[]{:S(2)}, u32[]{:S(2)}) %collective-permute-start.18) | collective-permute-done | bytes 2592 | tf_op jit(solution)/shard_map/ppermute | solution.py:176
  78.4 1.6 %collective-permute-start.19 = (f32[2,320]{1,0:T(2,128)S(1)}, f32[2,320]{1,0:T(2,128)S(1)}, u32[]{:S(2)}, u32[]{:S(2)}) collective-permute-start(f32[2,320]{1,0:T(2,128)S(1)} %add.106), channel_id=1, source_target_pairs={{0,1},{1,0},{2,3},{3,2},{4,5},{5,4},{6,7},{7,6},{8,9},{9,8},{10,11... | collective-permute-start | bytes 7688 | tf_op jit(solution)/shard_map/ppermute | solution.py:176
  80.0 2.0 %collective-permute-done.19 = f32[2,320]{1,0:T(2,128)S(1)} collective-permute-done((f32[2,320]{1,0:T(2,128)S(1)}, f32[2,320]{1,0:T(2,128)S(1)}, u32[]{:S(2)}, u32[]{:S(2)}) %collective-permute-start.19) | collective-permute-done | bytes 2592 | tf_op jit(solution)/shard_map/ppermute | solution.py:176
  82.0 2.6 %collective-permute-start.20 = (f32[2,320]{1,0:T(2,128)S(1)}, f32[2,320]{1,0:T(2,128)S(1)}, u32[]{:S(2)}, u32[]{:S(2)}) collective-permute-start(f32[2,320]{1,0:T(2,128)S(1)} %add.107), channel_id=1, source_target_pairs={{0,2},{1,3},{2,0},{3,1},{4,6},{5,7},{6,4},{7,5},{8,10},{9,11},{10,... | collective-permute-start | bytes 7688 | tf_op jit(solution)/shard_map/ppermute | solution.py:176
  84.7 1.9 %collective-permute-done.20 = f32[2,320]{1,0:T(2,128)S(1)} collective-permute-done((f32[2,320]{1,0:T(2,128)S(1)}, f32[2,320]{1,0:T(2,128)S(1)}, u32[]{:S(2)}, u32[]{:S(2)}) %collective-permute-start.20) | collective-permute-done | bytes 2592 | tf_op jit(solution)/shard_map/ppermute | solution.py:176
  86.8 1.3 %convert_add_fusion = f32[320,320]{1,0:T(8,128)S(1)} fusion(bf16[320,320]{1,0:T(8,128)(2,1)} %collective-permute-done.9, bf16[320,320]{1,0:T(8,128)(2,1)} %collective-permute-done.8, bf16[320,320]{1,0:T(8,128)(2,1)S(1)} %collective-permute-done.7, bf16[320,320]{1,0:T(8,128)(2,1)S(1)} %copy.59, f32[1280,320]{1,0:T(8,128)S(1)} %copy-done.4), kind=kLoop, calls=%fused_computation.2 | loop fusion | flops 819200 | bytes 1638400 | tf_op jit(solution)/shard_map/add | solution.py:377
  88.2 1.7 %collective-permute-start.10 = (bf16[80,320]{1,0:T(8,128)(2,1)S(1)}, bf16[80,320]{1,0:T(8,128)(2,1)S(1)}, u32[]{:S(2)}, u32[]{:S(2)}) collective-permute-start(bf16[80,320]{1,0:T(8,128)(2,1)S(1)} %get-tuple-element.47), channel_id=1, source_target_pairs={{0,1},{1,0},{2,3},{3,2},{4,5},{5,4},{6,7},{7,6},{8,9},{9,8},{10,11... | collective-permute-start | bytes 153608 | tf_op jit(solution)/shard_map/ppermute | solution.py:176
  89.8 2.5 %collective-permute-start.11 = (bf16[80,320]{1,0:T(8,128)(2,1)S(1)}, bf16[80,320]{1,0:T(8,128)(2,1)S(1)}, u32[]{:S(2)}, u32[]{:S(2)}) collective-permute-start(bf16[80,320]{1,0:T(8,128)(2,1)S(1)} %get-tuple-element.49), channel_id=1, source_target_pairs={{0,2},{1,3},{2,0},{3,1},{4,6},{5,7},{6,4},{7,5},{8,10},{9,11},{10,... | collective-permute-start | bytes 153608 | tf_op jit(solution)/shard_map/ppermute | solution.py:176
  92.7 2.9 %collective-permute-done.11 = bf16[80,320]{1,0:T(8,128)(2,1)S(1)} collective-permute-done((bf16[80,320]{1,0:T(8,128)(2,1)S(1)}, bf16[80,320]{1,0:T(8,128)(2,1)S(1)}, u32[]{:S(2)}, u32[]{:S(2)}) %collective-permute-start.11) | collective-permute-done | bytes 51232 | tf_op jit(solution)/shard_map/ppermute | solution.py:176
  95.6 2.9 %collective-permute-done.12 = bf16[80,320]{1,0:T(8,128)(2,1)S(1)} collective-permute-done((bf16[80,320]{1,0:T(8,128)(2,1)S(1)}, bf16[80,320]{1,0:T(8,128)(2,1)S(1)}, u32[]{:S(2)}, u32[]{:S(2)}) %collective-permute-start.12) | collective-permute-done | bytes 51232 | tf_op jit(solution)/shard_map/ppermute | solution.py:176
  99.3 2.1 %collective-permute-start.14 = (bf16[80,320]{1,0:T(8,128)(2,1)S(1)}, bf16[80,320]{1,0:T(8,128)(2,1)S(1)}, u32[]{:S(2)}, u32[]{:S(2)}) collective-permute-start(bf16[80,320]{1,0:T(8,128)(2,1)S(1)} %get-tuple-element.25), channel_id=1, source_target_pairs={{0,2},{1,3},{2,0},{3,1},{4,6},{5,7},{6,4},{7,5},{8,10},{9,11},{10,... | collective-permute-start | bytes 153608 | tf_op jit(solution)/shard_map/ppermute | solution.py:176
  101.4 2.3 %collective-permute-start.15 = (bf16[80,320]{1,0:T(8,128)(2,1)S(1)}, bf16[80,320]{1,0:T(8,128)(2,1)S(1)}, u32[]{:S(2)}, u32[]{:S(2)}) collective-permute-start(bf16[80,320]{1,0:T(8,128)(2,1)S(1)} %get-tuple-element.25), channel_id=1, source_target_pairs={{0,3},{1,2},{2,1},{3,0},{4,7},{5,6},{6,5},{7,4},{8,11},{9,10},{10,... | collective-permute-start | bytes 153608 | tf_op jit(solution)/shard_map/ppermute | solution.py:176
  104.4 3.0 %collective-permute-done.15 = bf16[80,320]{1,0:T(8,128)(2,1)S(1)} collective-permute-done((bf16[80,320]{1,0:T(8,128)(2,1)S(1)}, bf16[80,320]{1,0:T(8,128)(2,1)S(1)}, u32[]{:S(2)}, u32[]{:S(2)}) %collective-permute-start.15) | collective-permute-done | bytes 51232 | tf_op jit(solution)/shard_map/ppermute | solution.py:176
  (107 shorter events, 22.3 us)
Async XLA Ops:
  0.6 7.0 %copy-start.7 = (f32[80,320]{1,0:T(8,128)S(1)}, f32[80,320]{1,0:T(8,128)}, u32[]{:S(2)}) copy-start(f32[80,320]{1,0:T(8,128)} %param.17) | copy-start | bytes 307204
  0.7 7.0 %copy-start.8 = (f32[80,320]{1,0:T(8,128)S(1)}, f32[80,320]{1,0:T(8,128)}, u32[]{:S(2)}) copy-start(f32[80,320]{1,0:T(8,128)} %param.18) | copy-start | bytes 307204
  3.6 9.0 %collective-permute-start.3 = (bf16[320,320]{1,0:T(8,128)(2,1)S(1)}, bf16[320,320]{1,0:T(8,128)(2,1)S(1)}, u32[]{:S(2)}, u32[]{:S(2)}) collective-permute-start(bf16[320,320]{1,0:T(8,128)(2,1)S(1)} %pad_maximum_fusion.3), channel_id=1, source_target_pairs={{0,16},{4,20},{8,24},{12,28},{16,0},{20,4},{24,8},{28,12},{1,17},{... | collective-permute-start | bytes 614408 | tf_op jit(solution)/shard_map/ppermute | solution.py:176
  7.7 8.1 %collective-permute-start = (bf16[320,320]{1,0:T(8,128)(2,1)S(1)}, bf16[320,320]{1,0:T(8,128)(2,1)S(1)}, u32[]{:S(2)}, u32[]{:S(2)}) collective-permute-start(bf16[320,320]{1,0:T(8,128)(2,1)S(1)} %pad_maximum_fusion.2), channel_id=1, source_target_pairs={{0,8},{4,12},{8,0},{12,4},{16,24},{20,28},{24,16},{28,20},{1,9},{5... | collective-permute-start | bytes 614408 | tf_op jit(solution)/shard_map/ppermute | solution.py:176
  12.6 13.1 %collective-permute-start.4 = (bf16[640,320]{1,0:T(8,128)(2,1)S(1)}, bf16[640,320]{1,0:T(8,128)(2,1)S(1)}, u32[]{:S(2)}, u32[]{:S(2)}) collective-permute-start(bf16[640,320]{1,0:T(8,128)(2,1)S(1)} %pad_maximum_fusion.1), channel_id=1, source_target_pairs={{0,8},{4,12},{8,0},{12,4},{16,24},{20,28},{24,16},{28,20},{1,9},{5... | collective-permute-start | bytes 1228808 | tf_op jit(solution)/shard_map/ppermute | solution.py:176
  15.9 11.4 %collective-permute-start.1 = (bf16[640,320]{1,0:T(8,128)(2,1)S(1)}, bf16[640,320]{1,0:T(8,128)(2,1)}, u32[]{:S(2)}, u32[]{:S(2)}) collective-permute-start(bf16[640,320]{1,0:T(8,128)(2,1)S(1)} %pad_maximum_fusion), channel_id=1, source_target_pairs={{0,16},{4,20},{8,24},{12,28},{16,0},{20,4},{24,8},{28,12},{1,17},{... | collective-permute-start | bytes 1228808 | tf_op jit(solution)/shard_map/ppermute | solution.py:176
  26.4 8.0 %collective-permute-start.5 = (bf16[1280,320]{0,1:T(8,128)(2,1)S(1)}, bf16[1280,320]{0,1:T(8,128)(2,1)}, u32[]{:S(2)}, u32[]{:S(2)}) collective-permute-start(bf16[1280,320]{0,1:T(8,128)(2,1)S(1)} %copy.48), channel_id=1, source_target_pairs={{0,4},{4,0},{8,12},{12,8},{16,20},{20,16},{24,28},{28,24},{1,5},{5... | collective-permute-start | bytes 2457608 | tf_op jit(solution)/shard_map/ppermute | solution.py:176
  28.4 5.2 %copy-start.17 = (f32[320]{0:T(512)S(1)}, f32[320]{0:T(512)}, u32[]{:S(2)}) copy-start(f32[320]{0:T(512)} %param.25) | copy-start | bytes 3844
  29.7 6.3 %collective-permute-start.2 = (bf16[1280,320]{0,1:T(8,128)(2,1)}, bf16[1280,320]{0,1:T(8,128)(2,1)}, u32[]{:S(2)}, u32[]{:S(2)}) collective-permute-start(bf16[1280,320]{0,1:T(8,128)(2,1)} %copy.47), channel_id=1, source_target_pairs={{0,4},{4,0},{8,12},{12,8},{16,20},{20,16},{24,28},{28,24},{1,5},{5... | collective-permute-start | bytes 2457608 | tf_op jit(solution)/shard_map/ppermute | solution.py:176
  52.9 7.2 %copy-start.4 = (f32[1280,320]{1,0:T(8,128)S(1)}, f32[1280,320]{1,0:T(8,128)}, u32[]{:S(2)}) copy-start(f32[1280,320]{1,0:T(8,128)} %get-tuple-element.13) | copy-start | bytes 4915204
  52.9 2.7 %collective-permute-start.6 = (bf16[1280,320]{0,1:T(8,128)(2,1)}, bf16[1280,320]{0,1:T(8,128)(2,1)S(1)}, u32[]{:S(2)}, u32[]{:S(2)}) collective-permute-start(bf16[1280,320]{0,1:T(8,128)(2,1)} %copy.54), channel_id=1, source_target_pairs={{0,4},{4,0},{8,12},{12,8},{16,20},{20,16},{24,28},{28,24},{1,5},{5... | collective-permute-start | bytes 2457608 | tf_op jit(solution)/shard_map/ppermute | solution.py:176
  53.4 11.1 %collective-permute-start.16 = (f32[2,320]{1,0:T(2,128)S(1)}, f32[2,320]{1,0:T(2,128)S(1)}, u32[]{:S(2)}, u32[]{:S(2)}) collective-permute-start(f32[2,320]{1,0:T(2,128)S(1)} %slice.53), channel_id=1, source_target_pairs={{0,4},{4,0},{8,12},{12,8},{16,20},{20,16},{24,28},{28,24},{1,5},{5... | collective-permute-start | bytes 7688 | tf_op jit(solution)/shard_map/ppermute | solution.py:176
  61.0 25.8 %collective-permute-start.7 = (bf16[320,320]{1,0:T(8,128)(2,1)}, bf16[320,320]{1,0:T(8,128)(2,1)S(1)}, u32[]{:S(2)}, u32[]{:S(2)}) collective-permute-start(bf16[320,320]{1,0:T(8,128)(2,1)} %get-tuple-element.38), channel_id=1, source_target_pairs={{0,8},{4,12},{8,0},{12,4},{16,24},{20,28},{24,16},{28,20},{1,9},{5... | collective-permute-start | bytes 614408 | tf_op jit(solution)/shard_map/ppermute | solution.py:176
  62.5 24.3 %collective-permute-start.8 = (bf16[320,320]{1,0:T(8,128)(2,1)}, bf16[320,320]{1,0:T(8,128)(2,1)}, u32[]{:S(2)}, u32[]{:S(2)}) collective-permute-start(bf16[320,320]{1,0:T(8,128)(2,1)} %get-tuple-element.40), channel_id=1, source_target_pairs={{0,16},{4,20},{8,24},{12,28},{16,0},{20,4},{24,8},{28,12},{1,17},{... | collective-permute-start | bytes 614408 | tf_op jit(solution)/shard_map/ppermute | solution.py:176
  63.0 23.8 %collective-permute-start.9 = (bf16[320,320]{1,0:T(8,128)(2,1)}, bf16[320,320]{1,0:T(8,128)(2,1)}, u32[]{:S(2)}, u32[]{:S(2)}) collective-permute-start(bf16[320,320]{1,0:T(8,128)(2,1)} %get-tuple-element.39), channel_id=1, source_target_pairs={{0,24},{4,28},{8,16},{12,20},{16,8},{20,12},{24,0},{28,4},{1,25},{... | collective-permute-start | bytes 614408 | tf_op jit(solution)/shard_map/ppermute | solution.py:176
  64.5 10.3 %collective-permute-start.17 = (f32[2,320]{1,0:T(2,128)S(1)}, f32[2,320]{1,0:T(2,128)S(1)}, u32[]{:S(2)}, u32[]{:S(2)}) collective-permute-start(f32[2,320]{1,0:T(2,128)S(1)} %slice_add_fusion), channel_id=1, source_target_pairs={{0,8},{4,12},{8,0},{12,4},{16,24},{20,28},{24,16},{28,20},{1,9},{5... | collective-permute-start | bytes 7688 | tf_op jit(solution)/shard_map/ppermute | solution.py:176
  74.8 3.6 %collective-permute-start.18 = (f32[2,320]{1,0:T(2,128)S(1)}, f32[2,320]{1,0:T(2,128)S(1)}, u32[]{:S(2)}, u32[]{:S(2)}) collective-permute-start(f32[2,320]{1,0:T(2,128)S(1)} %add.105), channel_id=1, source_target_pairs={{0,16},{4,20},{8,24},{12,28},{16,0},{20,4},{24,8},{28,12},{1,17},{... | collective-permute-start | bytes 7688 | tf_op jit(solution)/shard_map/ppermute | solution.py:176
  78.4 3.6 %collective-permute-start.19 = (f32[2,320]{1,0:T(2,128)S(1)}, f32[2,320]{1,0:T(2,128)S(1)}, u32[]{:S(2)}, u32[]{:S(2)}) collective-permute-start(f32[2,320]{1,0:T(2,128)S(1)} %add.106), channel_id=1, source_target_pairs={{0,1},{1,0},{2,3},{3,2},{4,5},{5,4},{6,7},{7,6},{8,9},{9,8},{10,11... | collective-permute-start | bytes 7688 | tf_op jit(solution)/shard_map/ppermute | solution.py:176
  82.0 4.5 %collective-permute-start.20 = (f32[2,320]{1,0:T(2,128)S(1)}, f32[2,320]{1,0:T(2,128)S(1)}, u32[]{:S(2)}, u32[]{:S(2)}) collective-permute-start(f32[2,320]{1,0:T(2,128)S(1)} %add.107), channel_id=1, source_target_pairs={{0,2},{1,3},{2,0},{3,1},{4,6},{5,7},{6,4},{7,5},{8,10},{9,11},{10,... | collective-permute-start | bytes 7688 | tf_op jit(solution)/shard_map/ppermute | solution.py:176
  86.7 20.7 %copy-start.9 = (f32[80,320]{1,0:T(8,128)S(1)}, f32[80,320]{1,0:T(8,128)}, u32[]{:S(2)}) copy-start(f32[80,320]{1,0:T(8,128)} %param.18) | copy-start | bytes 307204
  86.8 20.7 %copy-start.10 = (f32[80,320]{1,0:T(8,128)S(1)}, f32[80,320]{1,0:T(8,128)}, u32[]{:S(2)}) copy-start(f32[80,320]{1,0:T(8,128)} %param.22) | copy-start | bytes 307204
  86.8 20.7 %copy-start.11 = (f32[80,320]{1,0:T(8,128)S(1)}, f32[80,320]{1,0:T(8,128)}, u32[]{:S(2)}) copy-start(f32[80,320]{1,0:T(8,128)} %param.23) | copy-start | bytes 307204
  88.1 20.2 %copy-start.5 = (f32[160,320]{1,0:T(8,128)S(1)}, f32[160,320]{1,0:T(8,128)}, u32[]{:S(2)}) copy-start(f32[160,320]{1,0:T(8,128)} %param.16) | copy-start | bytes 614404
  88.1 20.2 %copy-start.6 = (f32[160,320]{1,0:T(8,128)S(1)}, f32[160,320]{1,0:T(8,128)}, u32[]{:S(2)}) copy-start(f32[160,320]{1,0:T(8,128)} %param.21) | copy-start | bytes 614404
  88.2 4.5 %collective-permute-start.10 = (bf16[80,320]{1,0:T(8,128)(2,1)S(1)}, bf16[80,320]{1,0:T(8,128)(2,1)S(1)}, u32[]{:S(2)}, u32[]{:S(2)}) collective-permute-start(bf16[80,320]{1,0:T(8,128)(2,1)S(1)} %get-tuple-element.47), channel_id=1, source_target_pairs={{0,1},{1,0},{2,3},{3,2},{4,5},{5,4},{6,7},{7,6},{8,9},{9,8},{10,11... | collective-permute-start | bytes 153608 | tf_op jit(solution)/shard_map/ppermute | solution.py:176
  89.8 5.8 %collective-permute-start.11 = (bf16[80,320]{1,0:T(8,128)(2,1)S(1)}, bf16[80,320]{1,0:T(8,128)(2,1)S(1)}, u32[]{:S(2)}, u32[]{:S(2)}) collective-permute-start(bf16[80,320]{1,0:T(8,128)(2,1)S(1)} %get-tuple-element.49), channel_id=1, source_target_pairs={{0,2},{1,3},{2,0},{3,1},{4,6},{5,7},{6,4},{7,5},{8,10},{9,11},{10,... | collective-permute-start | bytes 153608 | tf_op jit(solution)/shard_map/ppermute | solution.py:176
  92.4 6.2 %collective-permute-start.12 = (bf16[80,320]{1,0:T(8,128)(2,1)S(1)}, bf16[80,320]{1,0:T(8,128)(2,1)S(1)}, u32[]{:S(2)}, u32[]{:S(2)}) collective-permute-start(bf16[80,320]{1,0:T(8,128)(2,1)S(1)} %get-tuple-element.48), channel_id=1, source_target_pairs={{0,3},{1,2},{2,1},{3,0},{4,7},{5,6},{6,5},{7,4},{8,11},{9,10},{10,... | collective-permute-start | bytes 153608 | tf_op jit(solution)/shard_map/ppermute | solution.py:176
  92.6 16.5 %copy-start.12 = (f32[320]{0:T(512)}, f32[320]{0:T(512)S(1)}, u32[]{:S(2)}) copy-start(f32[320]{0:T(512)S(1)} %get-tuple-element.16) | copy-start | bytes 3844
  92.6 16.5 %copy-start.13 = (f32[320]{0:T(512)}, f32[320]{0:T(512)S(1)}, u32[]{:S(2)}) copy-start(f32[320]{0:T(512)S(1)} %get-tuple-element.17) | copy-start | bytes 3844
  98.6 5.0 %collective-permute-start.13 = (bf16[80,320]{1,0:T(8,128)(2,1)S(1)}, bf16[80,320]{1,0:T(8,128)(2,1)S(1)}, u32[]{:S(2)}, u32[]{:S(2)}) collective-permute-start(bf16[80,320]{1,0:T(8,128)(2,1)S(1)} %get-tuple-element.25), channel_id=1, source_target_pairs={{0,1},{1,0},{2,3},{3,2},{4,5},{5,4},{6,7},{7,6},{8,9},{9,8},{10,11... | collective-permute-start | bytes 153608 | tf_op jit(solution)/shard_map/ppermute | solution.py:176
  99.3 5.1 %collective-permute-start.14 = (bf16[80,320]{1,0:T(8,128)(2,1)S(1)}, bf16[80,320]{1,0:T(8,128)(2,1)S(1)}, u32[]{:S(2)}, u32[]{:S(2)}) collective-permute-start(bf16[80,320]{1,0:T(8,128)(2,1)S(1)} %get-tuple-element.25), channel_id=1, source_target_pairs={{0,2},{1,3},{2,0},{3,1},{4,6},{5,7},{6,4},{7,5},{8,10},{9,11},{10,... | collective-permute-start | bytes 153608 | tf_op jit(solution)/shard_map/ppermute | solution.py:176
  101.4 6.0 %collective-permute-start.15 = (bf16[80,320]{1,0:T(8,128)(2,1)S(1)}, bf16[80,320]{1,0:T(8,128)(2,1)S(1)}, u32[]{:S(2)}, u32[]{:S(2)}) collective-permute-start(bf16[80,320]{1,0:T(8,128)(2,1)S(1)} %get-tuple-element.25), channel_id=1, source_target_pairs={{0,3},{1,2},{2,1},{3,0},{4,7},{5,6},{6,5},{7,4},{8,11},{9,10},{10,... | collective-permute-start | bytes 153608 | tf_op jit(solution)/shard_map/ppermute | solution.py:176
  (8 other events, 23.7 us)

commit v3 on v2

--- a/solution.py
+++ b/solution.py
@@ -4,6 +4,7 @@
 import jax.numpy as jnp
 from jax import lax
 from jax.experimental import pallas as pl
+from jax.experimental.layout import Layout, with_layout_constraint
 from jax.experimental.pallas import tpu as pltpu
 from jax.sharding import PartitionSpec as P
 
@@ -172,49 +173,197 @@
     )
 
 
+def row_major(x):
+    return with_layout_constraint(x, Layout(major_to_minor=(0, 1)))
+
+
 def exchange(x, axis, count, mask):
-    return lax.ppermute(x, axis, [(i, i ^ mask) for i in range(count)])
+    return row_major(lax.ppermute(row_major(x), axis, [(i, i ^ mask) for i in range(count)]))
 
 
 def gather_doubling(x, count, order):
-    masks = [0]
+    far = 1 << order[-1]
+    pieces, masks, found = x, [0], []
     for bit in order[:-1]:
-        x = jnp.concatenate([x, exchange(x, "dp", count, 1 << bit)])
-        masks = masks + [m ^ (1 << bit) for m in masks]
-    return x, exchange(x, "dp", count, 1 << order[-1]), masks, 1 << order[-1]
-
-
-def sum_over_rep(x, count):
-    me = lax.axis_index("rep")
-    rows = x.shape[0] // count
-    chunk = lambda k: lax.dynamic_slice_in_dim(x, (me ^ k) * rows, rows, axis=0)
-    total = chunk(0)
-    for k in range(1, count):
-        total = total + exchange(chunk(k).astype(jnp.bfloat16), "rep", count, k).astype(jnp.float32)
-    total = total.astype(jnp.bfloat16)
-    out = jnp.zeros(x.shape, jnp.float32)
-    for k in range(count):
-        got = exchange(total, "rep", count, k) if k else total
-        out = lax.dynamic_update_slice_in_dim(out, got.astype(jnp.float32), (me ^ k) * rows, axis=0)
-    return out
-
-
-def step_kernel(sizes, s_masks, s_far, t_masks, t_far):
+        got = exchange(pieces, "dp", count, 1 << bit)
+        got_masks = [m ^ (1 << bit) for m in masks]
+        if bit == order[-2]:
+            found.append((pieces, masks))
+            found.append((exchange(pieces, "dp", count, far), [m ^ far for m in masks]))
+            found.append((got, got_masks))
+            found.append((exchange(got, "dp", count, far), [m ^ far for m in got_masks]))
+        else:
+            pieces = jnp.concatenate([pieces, got])
+            masks = masks + got_masks
+    return [a for a, _ in found], [m for _, m in found]
+
+
+def split_rows(x):
+    high = x.astype(jnp.bfloat16)
+    low = (x - high.astype(jnp.float32)).astype(jnp.bfloat16)
+    return high, low, high.astype(jnp.float32) + low.astype(jnp.float32)
+
+
+def put_affine(ref, base, high, low):
+    pad = jnp.zeros((TAIL - 4, ref.shape[1]), jnp.float32)
+    rows = jnp.concatenate([high.astype(jnp.float32), low.astype(jnp.float32), pad], axis=0)
+    ref[base : base + TAIL, :] = rows.astype(jnp.bfloat16)
+
+
+def get_affine(ref, base):
+    rows = ref[base : base + TAIL, :].astype(jnp.float32)
+    return rows[0:2, :] + rows[2:4, :]
+
+
+def tree_sum(parts):
+    while len(parts) > 1:
+        parts = [parts[i] + parts[i + 1] for i in range(0, len(parts), 2)]
+    return parts[0]
+
+
+TAIL = 16
+SMALL = pltpu.CompilerParams(vmem_limit_bytes=8 * 1024 * 1024)
+VM = pl.BlockSpec(memory_space=pltpu.VMEM)
+SM = pl.BlockSpec(memory_space=pltpu.SMEM)
+
+
+def call(body, name, outs, inputs, scalars=0):
+    return pl.pallas_call(
+        body,
+        in_specs=[SM] * scalars + [VM] * (len(inputs) - scalars),
+        out_specs=[VM] * len(outs),
+        out_shape=[jax.ShapeDtypeStruct(shape, dtype) for shape, dtype in outs],
+        compiler_params=SMALL,
+        name=name,
+    )(*inputs)
+
+
+def chip_sums(keep, near, near_two, affine, rows, parts):
+    width = keep.shape[1]
+
+    split = parts // 2
+
+    def body(keep_ref, near_ref, two_ref, affine_ref, own_ref, held_ref, *sent):
+        own_ref[...] = keep_ref[:rows, :] + near_ref[:rows, :].astype(jnp.float32)
+        high, low, value = split_rows(affine_ref[0:2, :] + get_affine(near_ref, split * rows))
+        held_ref[...] = jnp.zeros_like(held_ref)
+        held_ref[0:2, :] = value
+        for k in range(1, parts):
+            at = slice(k * rows, (k + 1) * rows)
+            ref = near_ref if k < split else two_ref
+            base = (k if k < split else k - split) * rows
+            sent[k - 1][:rows, :] = (keep_ref[at, :] + ref[base : base + rows, :].astype(jnp.float32)).astype(jnp.bfloat16)
+            put_affine(sent[k - 1], rows, high, low)
+
+    outs = [((rows, width), jnp.float32), ((8, width), jnp.float32)]
+    outs += [((rows + TAIL, width), jnp.bfloat16)] * (parts - 1)
+    return call(body, "chip_sums", outs, [keep, near, near_two, affine])
+
+
+def plane_sums(me, own, held, got, parts):
+    rows, width = own.shape
+    size = rows // parts
+    n_got = len(got)
+
+    def body(me_ref, own_ref, held_ref, *refs):
+        got_refs, (mine_ref, next_ref), sent, (scratch,) = (
+            refs[:n_got], refs[n_got : n_got + 2], refs[n_got + 2 : -1], refs[-1:]
+        )
+        total = own_ref[...]
+        for ref in got_refs:
+            total = total + ref[:rows, :].astype(jnp.float32)
+        scratch[...] = total
+        summed = tree_sum([held_ref[0:2, :]] + [get_affine(ref, rows) for ref in got_refs])
+        high, low, value = split_rows(summed)
+        next_ref[...] = jnp.zeros_like(next_ref)
+        next_ref[0:2, :] = value
+        mine_ref[...] = scratch[pl.ds(pl.multiple_of(me_ref[0] * size, 8), size), :]
+        for k in range(1, parts):
+            at = pl.multiple_of((me_ref[0] ^ k) * size, 8)
+            sent[k - 1][:size, :] = scratch[pl.ds(at, size), :].astype(jnp.bfloat16)
+            put_affine(sent[k - 1], size, high, low)
+
+    outs = [((size, width), jnp.float32), ((8, width), jnp.float32)]
+    outs += [((size + TAIL, width), jnp.bfloat16)] * (parts - 1)
+    return pl.pallas_call(
+        body,
+        in_specs=[SM] + [VM] * (2 + n_got),
+        out_specs=[VM] * len(outs),
+        out_shape=[jax.ShapeDtypeStruct(shape, dtype) for shape, dtype in outs],
+        scratch_shapes=[pltpu.VMEM((rows, width), jnp.float32)],
+        compiler_params=SMALL,
+        name="plane_sums",
+    )(me, own, held, *got)
+
+
+def line_sums(mine, held, got):
+    size, width = mine.shape
+
+    def body(mine_ref, held_ref, *refs):
+        got_refs, (total_ref, affine_ref) = refs[:-2], refs[-2:]
+        total = mine_ref[...]
+        for ref in got_refs:
+            total = total + ref[:size, :].astype(jnp.float32)
+        total_ref[...] = total.astype(jnp.bfloat16)
+        affine_ref[...] = jnp.zeros_like(affine_ref)
+        affine_ref[0:2, :] = tree_sum([held_ref[0:2, :]] + [get_affine(ref, size) for ref in got_refs])
+
+    outs = [((size, width), jnp.bfloat16), ((8, width), jnp.float32)]
+    return call(body, "line_sums", outs, [mine, held] + list(got))
+
+
+def finish(me, pieces, students, targets):
+    size, width = pieces[0].shape
+    n_pieces = len(pieces)
+    n_nets = len(students)
+
+    def body(me_ref, *refs):
+        piece_refs = refs[:n_pieces]
+        s_refs = refs[n_pieces : n_pieces + n_nets]
+        t_refs = refs[n_pieces + n_nets : n_pieces + 2 * n_nets]
+        grads = refs[n_pieces + 2 * n_nets : n_pieces + 3 * n_nets]
+        news = refs[n_pieces + 3 * n_nets : n_pieces + 4 * n_nets]
+        scratch = refs[-1]
+        for k, ref in enumerate(piece_refs):
+            scratch[pl.ds(pl.multiple_of((me_ref[0] ^ k) * size, 8), size), :] = ref[...].astype(jnp.float32)
+        base = 0
+        for s_ref, t_ref, g_ref, n_ref in zip(s_refs, t_refs, grads, news):
+            grad = scratch[base : base + s_ref.shape[0], :]
+            base = base + s_ref.shape[0]
+            g_ref[...] = grad
+            n_ref[...] = ema_decay * t_ref[...] + (1.0 - ema_decay) * (s_ref[...] - learn_rate * grad)
+
+    outs = [jax.ShapeDtypeStruct(s.shape, jnp.float32) for s in students] * 2
+    return pl.pallas_call(
+        body,
+        in_specs=[SM] + [VM] * (n_pieces + 2 * n_nets),
+        out_specs=[VM] * len(outs),
+        out_shape=outs,
+        scratch_shapes=[pltpu.VMEM((size * n_pieces, width), jnp.float32)],
+        compiler_params=SMALL,
+        name="finish",
+    )(me, *pieces, *students, *targets)
+
+
+def step_kernel(sizes, s_masks, t_masks):
     count, in_rows, out_rows, time_rows, samples, tokens, width = sizes
     rows = in_rows + out_rows + time_rows
     hidden_count = out_rows * count
+    n_pieces = len(s_masks) + len(t_masks)
+    split = count // 4
 
     def body(
-        me_ref, s_tok, t_tok, s_feat, t_feat, s_feat_t, s_gain, s_bias, t_gain, t_bias,
-        s_near_ref, s_far_ref, t_near_ref, t_far_ref,
-        away_ref, keep_ref, affine_ref,
-        sw_in, sw_out, sw_time, tw_in, tw_out, tw_time, g_in, g_out, g_time, s_emb, t_emb, emb_grad,
+        me_ref, s_tok, t_tok, s_feat, t_feat, s_gain, s_bias, t_gain, t_bias, *rest
     ):
+        s_refs, t_refs, rest = rest[: len(s_masks)], rest[len(s_masks) : n_pieces], rest[n_pieces:]
+        (
+            away_ref, away_two_ref, keep_ref, affine_ref, sw_in, sw_out, sw_time, tw_in, tw_out, tw_time, g_in, g_out, g_time, s_emb, t_emb, emb_grad, affine,
+        ) = rest
         me = me_ref[0]
 
-        def place(ref, masks, flip, w_in, w_out, w_time):
+        def place(ref, masks, w_in, w_out, w_time):
             for p, mask in enumerate(masks):
-                at = me ^ (mask ^ flip)
+                at = me ^ mask
                 base = p * rows
                 w_in[pl.ds(pl.multiple_of(at * in_rows, 16), in_rows), :] = ref[base : base + in_rows, :]
                 base = base + in_rows
@@ -222,15 +371,16 @@
                 base = base + out_rows
                 w_time[pl.ds(pl.multiple_of(at * time_rows, 16), time_rows), :] = ref[base : base + time_rows, :]
 
-        place(s_near_ref, s_masks, 0, sw_in, sw_out, sw_time)
-        place(s_far_ref, s_masks, s_far, sw_in, sw_out, sw_time)
-        place(t_near_ref, t_masks, 0, tw_in, tw_out, tw_time)
-        place(t_far_ref, t_masks, t_far, tw_in, tw_out, tw_time)
+        for ref, masks in zip(s_refs, s_masks):
+            place(ref, masks, sw_in, sw_out, sw_time)
+        for ref, masks in zip(t_refs, t_masks):
+            place(ref, masks, tw_in, tw_out, tw_time)
         s_emb[...] = jnp.dot(s_feat[...], sw_time[...], preferred_element_type=jnp.float32)
         t_emb[...] = jnp.dot(t_feat[...], tw_time[...], preferred_element_type=jnp.float32)
         g_in[...] = jnp.zeros_like(g_in)
         g_out[...] = jnp.zeros_like(g_out)
-        affine_ref[...] = jnp.zeros_like(affine_ref)
+        affine[...] = jnp.zeros_like(affine)
+        emb_grad[...] = jnp.zeros_like(emb_grad)
 
         def norm(tok, emb, gain, bias):
             summed = tok.astype(jnp.float32) + emb
@@ -241,11 +391,11 @@
 
         for s in range(samples):
             at = slice(s * tokens, (s + 1) * tokens)
-            t_sum, _, _, t_norm = norm(t_tok[at, :], t_emb[s : s + 1, :], t_gain[...], t_bias[...])
+            t_sum, _, _, t_norm = norm(t_tok[:, at].T, t_emb[s : s + 1, :], t_gain[...], t_bias[...])
             t_mixed = contract_last(t_norm, tw_in[...])
             t_hidden = (gelu_tanh(t_mixed[:, :hidden_count]) * t_mixed[:, hidden_count:]).astype(jnp.bfloat16)
             t_res = t_sum + jnp.dot(t_hidden, tw_out[...], preferred_element_type=jnp.float32)
-            s_sum, normed, inv_std, normed_b = norm(s_tok[at, :], s_emb[s : s + 1, :], s_gain[...], s_bias[...])
+            s_sum, normed, inv_std, normed_b = norm(s_tok[:, at].T, s_emb[s : s + 1, :], s_gain[...], s_bias[...])
             mixed = contract_last(normed_b, sw_in[...])
             gate = mixed[:, :hidden_count]
             up = mixed[:, hidden_count:]
@@ -267,8 +417,8 @@
             grad_z = jnp.dot(mix_gate, sw_in[:hidden_count, :], preferred_element_type=jnp.float32) + jnp.dot(
                 mix_up, sw_in[hidden_count:, :], preferred_element_type=jnp.float32
             )
-            affine_ref[0:1, :] += jnp.sum(grad_z * normed, axis=0, keepdims=True)
-            affine_ref[1:2, :] += jnp.sum(grad_z, axis=0, keepdims=True)
+            affine[0:1, :] += jnp.sum(grad_z * normed, axis=0, keepdims=True)
+            affine[1:2, :] += jnp.sum(grad_z, axis=0, keepdims=True)
             grad_n = grad_z * s_gain[...]
             grad_s = grad_y + inv_std * (
                 grad_n
@@ -277,15 +427,24 @@
             )
             emb_grad[s : s + 1, :] = jnp.sum(grad_s, axis=0, keepdims=True)
 
-        total = s_feat_t[:, 0:1] * emb_grad[0:1, :]
-        for s in range(1, samples):
-            total = total + s_feat_t[:, s : s + 1] * emb_grad[s : s + 1, :]
+        rest_of = emb_grad[...]
+        total = jnp.zeros(g_time.shape, jnp.float32)
+        for _ in range(3):
+            piece = rest_of.astype(jnp.bfloat16)
+            rest_of = rest_of - piece.astype(jnp.float32)
+            total = total + contract_first(s_feat[...], piece)
         g_time[...] = total
+        high, low, value = split_rows(affine[0:2, :])
+        affine_ref[...] = jnp.zeros_like(affine_ref)
+        affine_ref[0:2, :] = value
+        put_affine(away_ref, split * rows, high, low)
 
         for p in range(count // 2):
             for flip, out in ((0, keep_ref), (1, away_ref)):
                 at = me ^ (2 * p + flip)
                 base = p * rows
+                if flip and p >= split:
+                    out, base = away_two_ref, (p - split) * rows
                 for ref, size in ((g_in, in_rows), (g_out, out_rows), (g_time, time_rows)):
                     out[base : base + size, :] = ref[pl.ds(pl.multiple_of(at * size, 16), size), :].astype(out.dtype)
                     base = base + size
@@ -295,10 +454,11 @@
     half = count // 2 * rows
     return pl.pallas_call(
         body,
-        in_specs=[pl.BlockSpec(memory_space=pltpu.SMEM)] + [vm] * 13,
-        out_specs=[vm] * 3,
+        in_specs=[pl.BlockSpec(memory_space=pltpu.SMEM)] + [vm] * (8 + n_pieces),
+        out_specs=[vm] * 4,
         out_shape=[
-            jax.ShapeDtypeStruct((half, width), bf16),
+            jax.ShapeDtypeStruct((split * rows + TAIL, width), bf16),
+            jax.ShapeDtypeStruct((half - split * rows, width), bf16),
             jax.ShapeDtypeStruct((half, width), f32),
             jax.ShapeDtypeStruct((8, width), f32),
         ],
@@ -314,9 +474,10 @@
             pltpu.VMEM((time_rows * count, width), f32),
             pltpu.VMEM((16, width), f32),
             pltpu.VMEM((16, width), f32),
+            pltpu.VMEM((16, width), f32),
             pltpu.VMEM((8, width), f32),
         ],
-        compiler_params=pltpu.CompilerParams(vmem_limit_bytes=48 * 1024 * 1024),
+        compiler_params=pltpu.CompilerParams(vmem_limit_bytes=28 * 1024 * 1024),
         name="distill_step",
     )
 
@@ -350,8 +511,8 @@
             block = jnp.concatenate([win, wout, wtime]).astype(jnp.bfloat16)
             return gather_doubling(block, n_dp, order)
 
-        s_near, s_far, s_masks, s_flip = net(student_win, student_wout, student_wtime, up)
-        t_near, t_far, t_masks, t_flip = net(target_win, target_wout, target_wtime, down)
+        s_pieces, s_masks = net(student_win, student_wout, student_wtime, up)
+        t_pieces, t_masks = net(target_win, target_wout, target_wtime, down)
 
         def feats(ids):
             feat = jax.nn.silu(sinusoid(ids, time_rows * n_dp)).astype(jnp.bfloat16)
@@ -361,30 +522,27 @@
         t_feat = feats(timesteps - SKIP)
         kernel = step_kernel(
             (n_dp, in_rows, out_rows, time_rows, samples, student_in.shape[0] // samples, width),
-            s_masks, s_flip, t_masks, t_flip,
+            s_masks, t_masks,
         )
-        away, keep, affine = kernel(
+        away, away_two, keep, affine = kernel(
             lax.axis_index("dp").reshape(1),
-            student_in, target_in, s_feat, t_feat, s_feat.astype(jnp.float32).T,
+            student_in.T, target_in.T, s_feat, t_feat,
             student_gain[None], student_bias[None], target_gain[None], target_bias[None],
-            s_near, s_far, t_near, t_far,
+            *s_pieces, *t_pieces,
         )
         near = exchange(away, "dp", n_dp, 1)
-        total = keep[:rows] + near[:rows].astype(jnp.float32)
-        for k in range(1, n_dp // 2):
-            at = slice(k * rows, (k + 1) * rows)
-            part = (keep[at] + near[at].astype(jnp.float32)).astype(jnp.bfloat16)
-            total = total + exchange(part, "dp", n_dp, 2 * k).astype(jnp.float32)
-        affine = affine[:2]
-        for bit in range(bits):
-            affine = affine + exchange(affine, "dp", n_dp, 1 << bit)
-        for bit in range(n_rep.bit_length() - 1):
-            affine = affine + exchange(affine, "rep", n_rep, 1 << bit)
-        total_gain, total_bias = affine[0], affine[1]
-        total = sum_over_rep(total, n_rep)
-        shard_in = total[:in_rows]
-        shard_out = total[in_rows : in_rows + out_rows]
-        shard_time = total[in_rows + out_rows :]
+        near_two = exchange(away_two, "dp", n_dp, 1)
+        own, held, *sent = chip_sums(keep, near, near_two, affine, rows, n_dp // 2)
+        got = [exchange(part, "dp", n_dp, 2 * k) for k, part in enumerate(sent, 1)]
+        rep_me = lax.axis_index("rep").reshape(1)
+        mine, held, *sent = plane_sums(rep_me, own, held, got, n_rep)
+        got = [exchange(part, "rep", n_rep, k) for k, part in enumerate(sent, 1)]
+        total, held = line_sums(mine, held, got)
+        pieces = [total] + [exchange(total, "rep", n_rep, k) for k in range(1, n_rep)]
+        total_gain, total_bias = held[0], held[1]
+        shard_in, shard_out, shard_time, new_in, new_out, new_time = finish(
+            rep_me, pieces, [student_win, student_wout, student_wtime], [target_win, target_wout, target_wtime]
+        )
 
         def average(target_p, student_p, grad_p):
             return ema_decay * target_p + (1.0 - ema_decay) * (student_p - learn_rate * grad_p)
@@ -395,9 +553,9 @@
             shard_time,
             total_gain,
             total_bias,
-            average(target_win, student_win, shard_in),
-            average(target_wout, student_wout, shard_out),
-            average(target_wtime, student_wtime, shard_time),
+            new_in,
+            new_out,
+            new_time,
             average(target_gain, student_gain, total_gain),
             average(target_bias, student_bias, total_bias),
         )

time: 110 us -> 76.4 us (0.69)
  local copies, waits for them, and re-layouts: 21.6 us -> 0.13 us
  starting transfers between devices: 26.1 us -> 20.1 us
  waiting for transfers between devices: 42.3 us -> 38.7 us
  other arithmetic: 9.71 us -> 7.21 us
    unnamed x47 -> x30, local copies, waits for them, and re-layouts: 11.1 us -> 0.08 us
    ppermute x21 -> x19, starting transfers between devices: 26.1 us -> 20.1 us  [exchange(): lax.ppermute(row_major(x), axis, [(i, i ^ mask) for i in range(count)])]
    another operation x0 -> x6, other arithmetic: none -> 5.59 us
    unnamed x6 -> x0, other arithmetic: 3.88 us -> none
    ppermute x2 -> x0, local copies, waits for them, and re-layouts: 3.8 us -> none  [exchange(): return lax.ppermute(x, axis, [(i, i ^ mask) for i in range(count)])]
    ppermute x21 -> x19, waiting for transfers between devices: 42.3 us -> 38.7 us  [exchange(): lax.ppermute(row_major(x), axis, [(i, i ^ mask) for i in range(count)])]
    concatenate x4 -> x0, local copies, waits for them, and re-layouts: 3.07 us -> none  [gather_doubling(): x = jnp.concatenate([x, exchange(x, 'dp', count, 1 << bit)])]
    pallas_call x1 -> x0, local copies, waits for them, and re-layouts: 2.2 us -> none  [paired(): kernel(lax.axis_index('dp').reshape(1), student_in, target_in, s_feat, t_...]
  transfers between devices with their start and end apart: 21 -> 19, of which waited for: 13 -> 14; matrix products, arithmetic and copies ran while one was open for 15% -> 6% of each run, Pallas kernels for 0% -> 0%
where the time goes in v3:
time: 76.4 us; the launch traced here: 76.2 us
  waiting for transfers between devices  38.7 us (51%)
  starting transfers between devices  20.1 us (26%)
  Pallas kernels  9.05 us (12%)
  other arithmetic  7.21 us (9%)
  between operations  0.96 us (1%)
    ppermute x19, waiting for transfers between devices, exchange(): lax.ppermute(row_major(x), axis, [(i, i ^ mask) for i in range(count)])  38.7 us
    ppermute x19, starting transfers between devices, exchange(): lax.ppermute(row_major(x), axis, [(i, i ^ mask) for i in range(count)])  20.1 us
    pallas_call x1, Pallas kernels, paired(): kernel(lax.axis_index('dp').reshape(1), student_in.T, target_in.T, s_feat...  7.57 us
    another operation x6, other arithmetic  5.59 us
  transfers between devices with their start and end apart: 19, of which 14 were waited for; matrix products, arithmetic and copies ran while one was open for 6% of the time, Pallas kernels for 0%

profile of v3, /device:TPU:0, one launch (start us, length us, event | category | flops | bytes accessed | tf_op | source)
XLA Modules:
  0.0 76.2 jit_solution(10508617695726471884)
XLA Ops:
  0.6 0.9 %convert.22 = bf16[80,320]{1,0:T(8,128)(2,1)S(1)} convert(f32[80,320]{1,0:T(8,128)} %refs_8_.1) | non-fusion elementwise | flops 25600 | bytes 153600 | tf_op jit(solution)/shard_map/convert.1
  1.6 0.9 %convert.23 = bf16[80,320]{1,0:T(8,128)(2,1)S(1)} convert(f32[80,320]{1,0:T(8,128)} %refs_9_.1) | non-fusion elementwise | flops 25600 | bytes 153600 | tf_op jit(solution)/shard_map/convert.2
  2.5 1.0 %convert.21 = bf16[160,320]{1,0:T(8,128)(2,1)S(1)} convert(f32[160,320]{1,0:T(8,128)} %refs_7_.1) | non-fusion elementwise | flops 51200 | bytes 307200 | tf_op jit(solution)/shard_map/convert
  3.6 3.1 %collective-permute-start.4 = (bf16[320,320]{1,0:T(8,128)(2,1)S(1)}, bf16[320,320]{1,0:T(8,128)(2,1)S(1)}, u32[]{:S(2)}, u32[]{:S(2)}) collective-permute-start(bf16[320,320]{1,0:T(8,128)(2,1)S(1)} %pad_maximum_fusion.3), channel_id=1, source_target_pairs={{0,16},{4,20},{8,24},{12,28},{16,0},{20,4},{24,8},{28,12},{1,17},{... | collective-permute-start | bytes 614408 | tf_op jit(solution)/shard_map/ppermute | solution.py:181
  6.6 0.9 %convert.19 = bf16[80,320]{1,0:T(8,128)(2,1)S(1)} convert(f32[80,320]{1,0:T(8,128)} %refs_5_.1) | non-fusion elementwise | flops 25600 | bytes 153600 | tf_op jit(solution)/shard_map/convert.4
  7.6 0.9 %convert.20 = bf16[80,320]{1,0:T(8,128)(2,1)S(1)} convert(f32[80,320]{1,0:T(8,128)} %refs_6_.1) | non-fusion elementwise | flops 25600 | bytes 153600 | tf_op jit(solution)/shard_map/convert.5
  8.5 1.0 %convert.18 = bf16[160,320]{1,0:T(8,128)(2,1)S(1)} convert(f32[160,320]{1,0:T(8,128)} %refs_4_.1) | non-fusion elementwise | flops 51200 | bytes 307200 | tf_op jit(solution)/shard_map/convert.3
  9.5 1.6 %collective-permute-start = (bf16[320,320]{1,0:T(8,128)(2,1)S(1)}, bf16[320,320]{1,0:T(8,128)(2,1)S(1)}, u32[]{:S(2)}, u32[]{:S(2)}) collective-permute-start(bf16[320,320]{1,0:T(8,128)(2,1)S(1)} %pad_maximum_fusion.2), channel_id=1, source_target_pairs={{0,8},{4,12},{8,0},{12,4},{16,24},{20,28},{24,16},{28,20},{1,9},{5... | collective-permute-start | bytes 614408 | tf_op jit(solution)/shard_map/ppermute | solution.py:181
  11.0 1.6 %collective-permute-done.4 = bf16[320,320]{1,0:T(8,128)(2,1)S(1)} collective-permute-done((bf16[320,320]{1,0:T(8,128)(2,1)S(1)}, bf16[320,320]{1,0:T(8,128)(2,1)S(1)}, u32[]{:S(2)}, u32[]{:S(2)}) %collective-permute-start.4) | collective-permute-done | bytes 204832 | tf_op jit(solution)/shard_map/ppermute | solution.py:181
  12.7 1.8 %collective-permute-start.6 = (bf16[640,320]{1,0:T(8,128)(2,1)S(1)}, bf16[640,320]{1,0:T(8,128)(2,1)S(1)}, u32[]{:S(2)}, u32[]{:S(2)}) collective-permute-start(bf16[640,320]{1,0:T(8,128)(2,1)S(1)} %pad_maximum_fusion.1.rest_4_), channel_id=1, source_target_pairs={{0,8},{4,12},{8,0},{12,4},{16,24},{20,28},{24,16},{28,20},{1,9},{5... | collective-permute-start | bytes 1228808 | tf_op jit(solution)/shard_map/ppermute | solution.py:181
  14.4 3.9 %collective-permute-done = bf16[320,320]{1,0:T(8,128)(2,1)S(1)} collective-permute-done((bf16[320,320]{1,0:T(8,128)(2,1)S(1)}, bf16[320,320]{1,0:T(8,128)(2,1)S(1)}, u32[]{:S(2)}, u32[]{:S(2)}) %collective-permute-start) | collective-permute-done | bytes 204832 | tf_op jit(solution)/shard_map/ppermute | solution.py:181
  19.2 8.3 %collective-permute-done.6.rest_6_ = bf16[640,320]{1,0:T(8,128)(2,1)S(1)} collective-permute-done((bf16[640,320]{1,0:T(8,128)(2,1)S(1)}, bf16[640,320]{1,0:T(8,128)(2,1)S(1)}, u32[]{:S(2)}, u32[]{:S(2)}) %collective-permute-start.6) | collective-permute-done | bytes 409632 | tf_op jit(solution)/shard_map/ppermute | solution.py:181
  27.5 1.4 %collective-permute-done.2.rest_2_ = bf16[640,320]{1,0:T(8,128)(2,1)S(1)} collective-permute-done((bf16[640,320]{1,0:T(8,128)(2,1)S(1)}, bf16[640,320]{1,0:T(8,128)(2,1)S(1)}, u32[]{:S(2)}, u32[]{:S(2)}) %collective-permute-start.2) | collective-permute-done | bytes 409632 | tf_op jit(solution)/shard_map/ppermute | solution.py:181
  29.4 1.4 %collective-permute-done.3.rest_3_ = bf16[640,320]{1,0:T(8,128)(2,1)S(1)} collective-permute-done((bf16[640,320]{1,0:T(8,128)(2,1)S(1)}, bf16[640,320]{1,0:T(8,128)(2,1)S(1)}, u32[]{:S(2)}, u32[]{:S(2)}) %collective-permute-start.3) | collective-permute-done | bytes 409632 | tf_op jit(solution)/shard_map/ppermute | solution.py:181
  30.8 7.6 %distill_step.1 = (bf16[656,320]{1,0:T(8,128)(2,1)S(1)}, bf16[640,320]{1,0:T(8,128)(2,1)S(1)}, f32[1280,320]{1,0:T(8,128)S(1)}, f32[8,320]{1,0:T(8,128)S(1)}) custom-call(s32[1]{0:T(128)} %bitcast.1.me_ref, bf16[320,512]{1,0:T(8,128)(2,1)S(1)} %bitcast.4, bf16[320,512]{1,0:T(8,128)(2,1)S(1)} %bitcast.5, bf16[16,640]{1,0:T(8,128)(2,1)S(1)} %pad.7.s_feat, ...), custom_call_target="tpu_custom_call" | custom-call | tf_op jit(solution)/shard_map/distill_step/pallas_call | solution.py:527
  38.9 2.1 %collective-permute-done.9.two_ref = bf16[640,320]{1,0:T(8,128)(2,1)S(1)} collective-permute-done((bf16[640,320]{1,0:T(8,128)(2,1)S(1)}, bf16[640,320]{1,0:T(8,128)(2,1)S(1)}, u32[]{:S(2)}, u32[]{:S(2)}) %collective-permute-start.9) | collective-permute-done | bytes 409632 | tf_op jit(solution)/shard_map/ppermute | solution.py:181
  41.3 1.6 %collective-permute-start.10 = (bf16[336,320]{1,0:T(8,128)(2,1)S(1)}, bf16[336,320]{1,0:T(8,128)(2,1)S(1)}, u32[]{:S(2)}, u32[]{:S(2)}) collective-permute-start(bf16[336,320]{1,0:T(8,128)(2,1)S(1)} %get-tuple-element.38), channel_id=1, source_target_pairs={{0,8},{4,12},{8,0},{12,4},{16,24},{20,28},{24,16},{28,20},{1,9},{5... | collective-permute-start | bytes 645128 | tf_op jit(solution)/shard_map/ppermute | solution.py:181
  43.3 1.5 %collective-permute-start.12 = (bf16[336,320]{1,0:T(8,128)(2,1)S(1)}, bf16[336,320]{1,0:T(8,128)(2,1)S(1)}, u32[]{:S(2)}, u32[]{:S(2)}) collective-permute-start(bf16[336,320]{1,0:T(8,128)(2,1)S(1)} %get-tuple-element.40), channel_id=1, source_target_pairs={{0,24},{4,28},{8,16},{12,20},{16,8},{20,12},{24,0},{28,4},{1,25},{... | collective-permute-start | bytes 645128 | tf_op jit(solution)/shard_map/ppermute | solution.py:181
  44.8 5.6 %collective-permute-done.10.refs_0_ = bf16[336,320]{1,0:T(8,128)(2,1)S(1)} collective-permute-done((bf16[336,320]{1,0:T(8,128)(2,1)S(1)}, bf16[336,320]{1,0:T(8,128)(2,1)S(1)}, u32[]{:S(2)}, u32[]{:S(2)}) %collective-permute-start.10) | collective-permute-done | bytes 215072 | tf_op jit(solution)/shard_map/ppermute | solution.py:181
  50.4 5.9 %collective-permute-done.11.refs_1_ = bf16[336,320]{1,0:T(8,128)(2,1)S(1)} collective-permute-done((bf16[336,320]{1,0:T(8,128)(2,1)S(1)}, bf16[336,320]{1,0:T(8,128)(2,1)S(1)}, u32[]{:S(2)}, u32[]{:S(2)}) %collective-permute-start.11) | collective-permute-done | bytes 215072 | tf_op jit(solution)/shard_map/ppermute | solution.py:181
  56.6 1.6 %collective-permute-start.13 = (bf16[96,320]{1,0:T(8,128)(2,1)S(1)}, bf16[96,320]{1,0:T(8,128)(2,1)S(1)}, u32[]{:S(2)}, u32[]{:S(2)}) collective-permute-start(bf16[96,320]{1,0:T(8,128)(2,1)S(1)} %get-tuple-element.43), channel_id=1, source_target_pairs={{0,1},{1,0},{2,3},{3,2},{4,5},{5,4},{6,7},{7,6},{8,9},{9,8},{10,11... | collective-permute-start | bytes 184328 | tf_op jit(solution)/shard_map/ppermute | solution.py:181
  58.2 2.6 %collective-permute-start.14 = (bf16[96,320]{1,0:T(8,128)(2,1)S(1)}, bf16[96,320]{1,0:T(8,128)(2,1)S(1)}, u32[]{:S(2)}, u32[]{:S(2)}) collective-permute-start(bf16[96,320]{1,0:T(8,128)(2,1)S(1)} %get-tuple-element.44), channel_id=1, source_target_pairs={{0,2},{1,3},{2,0},{3,1},{4,6},{5,7},{6,4},{7,5},{8,10},{9,11},{10,... | collective-permute-start | bytes 184328 | tf_op jit(solution)/shard_map/ppermute | solution.py:181
  61.0 0.7 collective-permute-done.13.refs_0_
  61.7 3.4 %collective-permute-done.14.refs_1_ = bf16[96,320]{1,0:T(8,128)(2,1)S(1)} collective-permute-done((bf16[96,320]{1,0:T(8,128)(2,1)S(1)}, bf16[96,320]{1,0:T(8,128)(2,1)S(1)}, u32[]{:S(2)}, u32[]{:S(2)}) %collective-permute-start.14) | collective-permute-done | bytes 61472 | tf_op jit(solution)/shard_map/ppermute | solution.py:181
  65.1 1.9 %collective-permute-done.15.refs_2_ = bf16[96,320]{1,0:T(8,128)(2,1)S(1)} collective-permute-done((bf16[96,320]{1,0:T(8,128)(2,1)S(1)}, bf16[96,320]{1,0:T(8,128)(2,1)S(1)}, u32[]{:S(2)}, u32[]{:S(2)}) %collective-permute-start.15) | collective-permute-done | bytes 61472 | tf_op jit(solution)/shard_map/ppermute | solution.py:181
  67.1 1.3 %collective-permute-start.17 = (bf16[80,320]{1,0:T(8,128)(2,1)S(1)}, bf16[80,320]{1,0:T(8,128)(2,1)S(1)}, u32[]{:S(2)}, u32[]{:S(2)}) collective-permute-start(bf16[80,320]{1,0:T(8,128)(2,1)S(1)} %get-tuple-element.46.refs_0_), channel_id=1, source_target_pairs={{0,2},{1,3},{2,0},{3,1},{4,6},{5,7},{6,4},{7,5},{8,10},{9,11},{10,... | collective-permute-start | bytes 153608 | tf_op jit(solution)/shard_map/ppermute | solution.py:181
  68.4 0.7 collective-permute-start.16
  69.1 2.5 %collective-permute-start.18 = (bf16[80,320]{1,0:T(8,128)(2,1)S(1)}, bf16[80,320]{1,0:T(8,128)(2,1)S(1)}, u32[]{:S(2)}, u32[]{:S(2)}) collective-permute-start(bf16[80,320]{1,0:T(8,128)(2,1)S(1)} %get-tuple-element.46.refs_0_), channel_id=1, source_target_pairs={{0,3},{1,2},{2,1},{3,0},{4,7},{5,6},{6,5},{7,4},{8,11},{9,10},{10,... | collective-permute-start | bytes 153608 | tf_op jit(solution)/shard_map/ppermute | solution.py:181
  71.6 0.6 multiply_add_fusion
  72.2 0.6 multiply_add_fusion.1
  73.0 2.1 %collective-permute-done.18.refs_3_ = bf16[80,320]{1,0:T(8,128)(2,1)S(1)} collective-permute-done((bf16[80,320]{1,0:T(8,128)(2,1)S(1)}, bf16[80,320]{1,0:T(8,128)(2,1)S(1)}, u32[]{:S(2)}, u32[]{:S(2)}) %collective-permute-start.18) | collective-permute-done | bytes 51232 | tf_op jit(solution)/shard_map/ppermute | solution.py:181
  75.1 1.0 %finish.1 = (f32[160,320]{1,0:T(8,128)}, f32[80,320]{1,0:T(8,128)}, f32[80,320]{1,0:T(8,128)}, f32[160,320]{1,0:T(8,128)}, f32[80,320]{1,0:T(8,128)}, /*index=5*/f32[80,320]{1,0:T(8,128)}) custom-call(s32[1]{0:T(128)} %bitcast.me_ref, bf16[80,320]{1,0:T(8,128)(2,1)S(1)} %get-tuple-element.46.refs_0_, bf16[80,320]{1,0:T(8,128)(2,1)S(1)} %collective-permute-done.16.refs_1_, ...), custom_call_target="tpu_custom_call" | custom-call | tf_op jit(solution)/shard_map/finish/pallas_call | solution.py:337
  (64 shorter events, 3.4 us)
Async XLA Ops:
  2.5 16.1 %copy-start.10 = (f32[320]{0:T(512)S(1)}, f32[320]{0:T(512)}, u32[]{:S(2)}) copy-start(f32[320]{0:T(512)} %param.19) | copy-start | bytes 3844
  2.5 16.1 %copy-start.8 = (f32[320]{0:T(512)S(1)}, f32[320]{0:T(512)}, u32[]{:S(2)}) copy-start(f32[320]{0:T(512)} %param.20) | copy-start | bytes 3844
  2.5 16.1 %copy-start.11 = (f32[320]{0:T(512)S(1)}, f32[320]{0:T(512)}, u32[]{:S(2)}) copy-start(f32[320]{0:T(512)} %param.24) | copy-start | bytes 3844
  2.5 16.1 %copy-start.9 = (f32[320]{0:T(512)S(1)}, f32[320]{0:T(512)}, u32[]{:S(2)}) copy-start(f32[320]{0:T(512)} %param.25) | copy-start | bytes 3844
  2.5 16.1 %copy-start.14 = (s32[2]{0:T(128)S(1)}, s32[2]{0:T(128)}, u32[]{:S(2)}) copy-start(s32[2]{0:T(128)} %param.15) | copy-start | bytes 28
  3.5 27.3 %copy-start.6 = (bf16[512,320]{0,1:T(8,128)(2,1)S(1)}, bf16[512,320]{0,1:T(8,128)(2,1)}, u32[]{:S(2)}) copy-start(bf16[512,320]{0,1:T(8,128)(2,1)} %param.13) | copy-start | bytes 983044
  3.5 27.2 %copy-start.7 = (bf16[512,320]{0,1:T(8,128)(2,1)S(1)}, bf16[512,320]{0,1:T(8,128)(2,1)}, u32[]{:S(2)}) copy-start(bf16[512,320]{0,1:T(8,128)(2,1)} %param.14) | copy-start | bytes 983044
  3.6 9.0 %collective-permute-start.4 = (bf16[320,320]{1,0:T(8,128)(2,1)S(1)}, bf16[320,320]{1,0:T(8,128)(2,1)S(1)}, u32[]{:S(2)}, u32[]{:S(2)}) collective-permute-start(bf16[320,320]{1,0:T(8,128)(2,1)S(1)} %pad_maximum_fusion.3), channel_id=1, source_target_pairs={{0,16},{4,20},{8,24},{12,28},{16,0},{20,4},{24,8},{28,12},{1,17},{... | collective-permute-start | bytes 614408 | tf_op jit(solution)/shard_map/ppermute | solution.py:181
  9.5 8.9 %collective-permute-start = (bf16[320,320]{1,0:T(8,128)(2,1)S(1)}, bf16[320,320]{1,0:T(8,128)(2,1)S(1)}, u32[]{:S(2)}, u32[]{:S(2)}) collective-permute-start(bf16[320,320]{1,0:T(8,128)(2,1)S(1)} %pad_maximum_fusion.2), channel_id=1, source_target_pairs={{0,8},{4,12},{8,0},{12,4},{16,24},{20,28},{24,16},{28,20},{1,9},{5... | collective-permute-start | bytes 614408 | tf_op jit(solution)/shard_map/ppermute | solution.py:181
  12.7 14.8 %collective-permute-start.6 = (bf16[640,320]{1,0:T(8,128)(2,1)S(1)}, bf16[640,320]{1,0:T(8,128)(2,1)S(1)}, u32[]{:S(2)}, u32[]{:S(2)}) collective-permute-start(bf16[640,320]{1,0:T(8,128)(2,1)S(1)} %pad_maximum_fusion.1.rest_4_), channel_id=1, source_target_pairs={{0,8},{4,12},{8,0},{12,4},{16,24},{20,28},{24,16},{28,20},{1,9},{5... | collective-permute-start | bytes 1228808 | tf_op jit(solution)/shard_map/ppermute | solution.py:181
  18.4 10.5 %collective-permute-start.2 = (bf16[640,320]{1,0:T(8,128)(2,1)S(1)}, bf16[640,320]{1,0:T(8,128)(2,1)S(1)}, u32[]{:S(2)}, u32[]{:S(2)}) collective-permute-start(bf16[640,320]{1,0:T(8,128)(2,1)S(1)} %pad_maximum_fusion.rest_0_), channel_id=1, source_target_pairs={{0,16},{4,20},{8,24},{12,28},{16,0},{20,4},{24,8},{28,12},{1,17},{... | collective-permute-start | bytes 1228808 | tf_op jit(solution)/shard_map/ppermute | solution.py:181
  18.6 10.6 %collective-permute-start.5 = (bf16[640,320]{1,0:T(8,128)(2,1)S(1)}, bf16[640,320]{1,0:T(8,128)(2,1)S(1)}, u32[]{:S(2)}, u32[]{:S(2)}) collective-permute-start(bf16[640,320]{1,0:T(8,128)(2,1)S(1)} %pad_maximum_fusion.1.rest_4_), channel_id=1, source_target_pairs={{0,4},{4,0},{8,12},{12,8},{16,20},{20,16},{24,28},{28,24},{1,5},{5... | collective-permute-start | bytes 1228808 | tf_op jit(solution)/shard_map/ppermute | solution.py:181
  18.7 10.5 %collective-permute-start.1 = (bf16[640,320]{1,0:T(8,128)(2,1)S(1)}, bf16[640,320]{1,0:T(8,128)(2,1)S(1)}, u32[]{:S(2)}, u32[]{:S(2)}) collective-permute-start(bf16[640,320]{1,0:T(8,128)(2,1)S(1)} %pad_maximum_fusion.rest_0_), channel_id=1, source_target_pairs={{0,4},{4,0},{8,12},{12,8},{16,20},{20,16},{24,28},{28,24},{1,5},{5... | collective-permute-start | bytes 1228808 | tf_op jit(solution)/shard_map/ppermute | solution.py:181
  27.5 1.9 %collective-permute-start.7 = (bf16[640,320]{1,0:T(8,128)(2,1)S(1)}, bf16[640,320]{1,0:T(8,128)(2,1)S(1)}, u32[]{:S(2)}, u32[]{:S(2)}) collective-permute-start(bf16[640,320]{1,0:T(8,128)(2,1)S(1)} %collective-permute-done.6.rest_6_), channel_id=1, source_target_pairs={{0,4},{4,0},{8,12},{12,8},{16,20},{20,16},{24,28},{28,24},{1,5},{5... | collective-permute-start | bytes 1228808 | tf_op jit(solution)/shard_map/ppermute | solution.py:181
  28.9 1.9 %collective-permute-start.3 = (bf16[640,320]{1,0:T(8,128)(2,1)S(1)}, bf16[640,320]{1,0:T(8,128)(2,1)S(1)}, u32[]{:S(2)}, u32[]{:S(2)}) collective-permute-start(bf16[640,320]{1,0:T(8,128)(2,1)S(1)} %collective-permute-done.2.rest_2_), channel_id=1, source_target_pairs={{0,4},{4,0},{8,12},{12,8},{16,20},{20,16},{24,28},{28,24},{1,5},{5... | collective-permute-start | bytes 1228808 | tf_op jit(solution)/shard_map/ppermute | solution.py:181
  38.4 2.7 %collective-permute-start.8 = (bf16[656,320]{1,0:T(8,128)(2,1)S(1)}, bf16[656,320]{1,0:T(8,128)(2,1)S(1)}, u32[]{:S(2)}, u32[]{:S(2)}) collective-permute-start(bf16[656,320]{1,0:T(8,128)(2,1)S(1)} %get-tuple-element.33), channel_id=1, source_target_pairs={{0,4},{4,0},{8,12},{12,8},{16,20},{20,16},{24,28},{28,24},{1,5},{5... | collective-permute-start | bytes 1259528 | tf_op jit(solution)/shard_map/ppermute | solution.py:181
  38.5 2.5 %collective-permute-start.9 = (bf16[640,320]{1,0:T(8,128)(2,1)S(1)}, bf16[640,320]{1,0:T(8,128)(2,1)S(1)}, u32[]{:S(2)}, u32[]{:S(2)}) collective-permute-start(bf16[640,320]{1,0:T(8,128)(2,1)S(1)} %get-tuple-element.34), channel_id=1, source_target_pairs={{0,4},{4,0},{8,12},{12,8},{16,20},{20,16},{24,28},{28,24},{1,5},{5... | collective-permute-start | bytes 1228808 | tf_op jit(solution)/shard_map/ppermute | solution.py:181
  41.0 34.1 %copy-start = (f32[160,320]{1,0:T(8,128)S(1)}, f32[160,320]{1,0:T(8,128)}, u32[]{:S(2)}) copy-start(f32[160,320]{1,0:T(8,128)} %refs_4_.1) | copy-start | bytes 614404
  41.0 34.1 %copy-start.1 = (f32[160,320]{1,0:T(8,128)S(1)}, f32[160,320]{1,0:T(8,128)}, u32[]{:S(2)}) copy-start(f32[160,320]{1,0:T(8,128)} %refs_7_.1) | copy-start | bytes 614404
  41.0 34.1 %copy-start.2 = (f32[80,320]{1,0:T(8,128)S(1)}, f32[80,320]{1,0:T(8,128)}, u32[]{:S(2)}) copy-start(f32[80,320]{1,0:T(8,128)} %refs_6_.1) | copy-start | bytes 307204
  41.0 34.1 %copy-start.3 = (f32[80,320]{1,0:T(8,128)S(1)}, f32[80,320]{1,0:T(8,128)}, u32[]{:S(2)}) copy-start(f32[80,320]{1,0:T(8,128)} %refs_5_.1) | copy-start | bytes 307204
  41.0 34.1 %copy-start.4 = (f32[80,320]{1,0:T(8,128)S(1)}, f32[80,320]{1,0:T(8,128)}, u32[]{:S(2)}) copy-start(f32[80,320]{1,0:T(8,128)} %refs_9_.1) | copy-start | bytes 307204
  41.0 34.1 %copy-start.5 = (f32[80,320]{1,0:T(8,128)S(1)}, f32[80,320]{1,0:T(8,128)}, u32[]{:S(2)}) copy-start(f32[80,320]{1,0:T(8,128)} %refs_8_.1) | copy-start | bytes 307204
  41.3 9.2 %collective-permute-start.10 = (bf16[336,320]{1,0:T(8,128)(2,1)S(1)}, bf16[336,320]{1,0:T(8,128)(2,1)S(1)}, u32[]{:S(2)}, u32[]{:S(2)}) collective-permute-start(bf16[336,320]{1,0:T(8,128)(2,1)S(1)} %get-tuple-element.38), channel_id=1, source_target_pairs={{0,8},{4,12},{8,0},{12,4},{16,24},{20,28},{24,16},{28,20},{1,9},{5... | collective-permute-start | bytes 645128 | tf_op jit(solution)/shard_map/ppermute | solution.py:181
  42.8 13.5 %collective-permute-start.11 = (bf16[336,320]{1,0:T(8,128)(2,1)S(1)}, bf16[336,320]{1,0:T(8,128)(2,1)S(1)}, u32[]{:S(2)}, u32[]{:S(2)}) collective-permute-start(bf16[336,320]{1,0:T(8,128)(2,1)S(1)} %get-tuple-element.39), channel_id=1, source_target_pairs={{0,16},{4,20},{8,24},{12,28},{16,0},{20,4},{24,8},{28,12},{1,17},{... | collective-permute-start | bytes 645128 | tf_op jit(solution)/shard_map/ppermute | solution.py:181
  43.3 13.0 %collective-permute-start.12 = (bf16[336,320]{1,0:T(8,128)(2,1)S(1)}, bf16[336,320]{1,0:T(8,128)(2,1)S(1)}, u32[]{:S(2)}, u32[]{:S(2)}) collective-permute-start(bf16[336,320]{1,0:T(8,128)(2,1)S(1)} %get-tuple-element.40), channel_id=1, source_target_pairs={{0,24},{4,28},{8,16},{12,20},{16,8},{20,12},{24,0},{28,4},{1,25},{... | collective-permute-start | bytes 645128 | tf_op jit(solution)/shard_map/ppermute | solution.py:181
  56.6 5.1 %collective-permute-start.13 = (bf16[96,320]{1,0:T(8,128)(2,1)S(1)}, bf16[96,320]{1,0:T(8,128)(2,1)S(1)}, u32[]{:S(2)}, u32[]{:S(2)}) collective-permute-start(bf16[96,320]{1,0:T(8,128)(2,1)S(1)} %get-tuple-element.43), channel_id=1, source_target_pairs={{0,1},{1,0},{2,3},{3,2},{4,5},{5,4},{6,7},{7,6},{8,9},{9,8},{10,11... | collective-permute-start | bytes 184328 | tf_op jit(solution)/shard_map/ppermute | solution.py:181
  58.2 6.9 %collective-permute-start.14 = (bf16[96,320]{1,0:T(8,128)(2,1)S(1)}, bf16[96,320]{1,0:T(8,128)(2,1)S(1)}, u32[]{:S(2)}, u32[]{:S(2)}) collective-permute-start(bf16[96,320]{1,0:T(8,128)(2,1)S(1)} %get-tuple-element.44), channel_id=1, source_target_pairs={{0,2},{1,3},{2,0},{3,1},{4,6},{5,7},{6,4},{7,5},{8,10},{9,11},{10,... | collective-permute-start | bytes 184328 | tf_op jit(solution)/shard_map/ppermute | solution.py:181
  60.8 6.3 %collective-permute-start.15 = (bf16[96,320]{1,0:T(8,128)(2,1)S(1)}, bf16[96,320]{1,0:T(8,128)(2,1)S(1)}, u32[]{:S(2)}, u32[]{:S(2)}) collective-permute-start(bf16[96,320]{1,0:T(8,128)(2,1)S(1)} %get-tuple-element.45), channel_id=1, source_target_pairs={{0,3},{1,2},{2,1},{3,0},{4,7},{5,6},{6,5},{7,4},{8,11},{9,10},{10,... | collective-permute-start | bytes 184328 | tf_op jit(solution)/shard_map/ppermute | solution.py:181
  67.1 5.7 %collective-permute-start.17 = (bf16[80,320]{1,0:T(8,128)(2,1)S(1)}, bf16[80,320]{1,0:T(8,128)(2,1)S(1)}, u32[]{:S(2)}, u32[]{:S(2)}) collective-permute-start(bf16[80,320]{1,0:T(8,128)(2,1)S(1)} %get-tuple-element.46.refs_0_), channel_id=1, source_target_pairs={{0,2},{1,3},{2,0},{3,1},{4,6},{5,7},{6,4},{7,5},{8,10},{9,11},{10,... | collective-permute-start | bytes 153608 | tf_op jit(solution)/shard_map/ppermute | solution.py:181
  68.4 4.6 %collective-permute-start.16 = (bf16[80,320]{1,0:T(8,128)(2,1)S(1)}, bf16[80,320]{1,0:T(8,128)(2,1)S(1)}, u32[]{:S(2)}, u32[]{:S(2)}) collective-permute-start(bf16[80,320]{1,0:T(8,128)(2,1)S(1)} %get-tuple-element.46.refs_0_), channel_id=1, source_target_pairs={{0,1},{1,0},{2,3},{3,2},{4,5},{5,4},{6,7},{7,6},{8,9},{9,8},{10,11... | collective-permute-start | bytes 153608 | tf_op jit(solution)/shard_map/ppermute | solution.py:181
  69.1 6.0 %collective-permute-start.18 = (bf16[80,320]{1,0:T(8,128)(2,1)S(1)}, bf16[80,320]{1,0:T(8,128)(2,1)S(1)}, u32[]{:S(2)}, u32[]{:S(2)}) collective-permute-start(bf16[80,320]{1,0:T(8,128)(2,1)S(1)} %get-tuple-element.46.refs_0_), channel_id=1, source_target_pairs={{0,3},{1,2},{2,1},{3,0},{4,7},{5,6},{6,5},{7,4},{8,11},{9,10},{10,... | collective-permute-start | bytes 153608 | tf_op jit(solution)/shard_map/ppermute | solution.py:181
  (2 other events, 9.2 us)
